TPU v7x, 128 devices: a whole 4x4x4 slice. The times are simulated.
128 devices in a mesh: client: 32 (over z, x, core), head: 4 (over y).
Axes of the slice: x: 4, y: 4, z: 4, core: 2. Of those that a mesh axis runs over, the one named last changes fastest.
Arguments:
- pre: bfloat16 [40960, 4096], P('client'), may hold values from -40 to 40
- delta: float32 [40960, 4096], P('client', 'head'), may hold values from -300 to 300
- head_weight: bfloat16 [4096, 4096], P(None, 'head'), may hold values from -0.09375 to 0.09375
- client_ids: int32 [512], P('client'), may hold values from 0 to 511, as said below
Outputs:
- head_grad: float32 [4096, 4096], P('client', 'head')
- bias_grad: float32 [4096], P('head')
- embed_grad: float32 [512, 4096], P('client', 'head')
- span_grad: float32 [80, 4096], P(None, 'head')
Inputs may be any that keep to these rules, and one draw needn't show every extreme that they name: `client_ids`: each of the 512 clients appears exactly once.
All inputs are finite; a program needn't handle non-finite values.
Results may differ from a plain program's by a relative error of at most 0.024.
Values may be sent and summed in bfloat16 or wider, within the bound.
A program may use at most 128 MiB of HBM per device.

v0:
```python
import jax
import jax.numpy as jnp
from jax import lax
from jax.sharding import Mesh
from jax.sharding import PartitionSpec as P

CLIENT = ("client_0", "client_1", "client_2")


EPSILON = 1e-06


def cut_along(x, dim, peers):
    before, after = (x.shape[:dim], x.shape[dim + 1 :])
    return jnp.moveaxis(x.reshape(*before, peers, -1, *after), dim, 0)


def sum_at_owner(x, axis, dim):
    tiles = cut_along(x, dim, lax.axis_size(axis))
    arrived = lax.all_to_all(tiles, axis, split_axis=0, concat_axis=0, tiled=True)
    return arrived.astype(jnp.float32).sum(axis=0)


def side_by_side(arrays, axis, dim, along):
    ends, at = ([], 0)
    for a in arrays[:-1]:
        at += a.shape[along]
        ends.append(at)
    both = jnp.concatenate(arrays, axis=along)
    return tuple(jnp.split(sum_at_owner(both, axis, dim), ends, axis=along))


def padded_to(lines, peers):
    spare = -len(lines) % peers
    return jnp.pad(lines, [(0, spare)] + [(0, 0)] * (lines.ndim - 1))


def joined_along(tiles, dim):
    shape = list(tiles.shape[1:])
    shape[dim] *= tiles.shape[0]
    return jnp.moveaxis(tiles, 0, dim).reshape(shape)


def sent_to_all(x, axis):
    peers = lax.axis_size(axis)
    return lax.all_to_all(jnp.broadcast_to(x[None], (peers, *x.shape)), axis, 0, 0, tiled=True)


def collect(x, axis, dim):
    return joined_along(sent_to_all(x, axis), dim)


def sum_by_parts(x, axes):
    lines = x.reshape(-1)
    padded = padded_to(lines, lax.axis_size(axes))
    whole = collect(sum_at_owner(padded, axes, 0).astype(jnp.bfloat16), axes, 0)
    return lax.slice_in_dim(whole, 0, len(lines)).reshape(x.shape).astype(jnp.float32)


def of_everyone(x, axis):
    return sent_to_all(x, axis).sum(axis=0)


def by_axis(x, axes):
    far, near = axes
    return of_everyone(of_everyone(x, near), far)


def in_one(arrays, axis):
    ends = [0]
    for a in arrays:
        ends.append(ends[-1] + a.size)
    subtotal = by_axis(jnp.concatenate([a.ravel() for a in arrays]), axis)
    return tuple((subtotal[b:e].reshape(a.shape) for a, b, e in zip(arrays, ends, ends[1:])))


def silu_slope(values):
    sigma = jax.nn.sigmoid(values)
    return sigma * (1.0 + values * (1.0 - sigma))


def clip_factor(total, number):
    return jnp.minimum(1.0, 1.0 / jnp.sqrt(total / number + EPSILON))


def per_device(pre, delta, head_weight, client_ids):
    rows_here, hidden_width = pre.shape
    emit_here = delta.shape[1]
    clients_here = client_ids.shape[0]
    span_count = rows_here // clients_here
    head_devices = lax.axis_size("head")
    client_devices = lax.axis_size(CLIENT)
    hidden = jax.nn.silu(pre.astype(jnp.float32)).astype(jnp.bfloat16)
    delta_low = delta.astype(jnp.bfloat16)
    head_raw = lax.psum_scatter(
        lax.dot_general(
            hidden, delta_low, (((0,), (0,)), ((), ())), preferred_element_type=jnp.float32
        ).astype(jnp.bfloat16),
        CLIENT,
        scatter_dimension=0,
        tiled=True,
    ).astype(jnp.float32)
    head_square = jnp.sum(head_raw * head_raw)
    bias_local = jnp.sum(delta, axis=0)
    partial_sum = lax.dot_general(
        delta_low, head_weight, (((1,), (1,)), ((), ())), preferred_element_type=jnp.float32
    )
    rounded = lax.optimization_barrier(partial_sum.astype(jnp.bfloat16))
    block_grad = rounded.astype(jnp.float32) * silu_slope(pre.astype(jnp.float32))
    grouped = block_grad.reshape(clients_here, span_count, hidden_width)
    client_whole = jnp.sum(grouped, axis=1)
    span_whole = jnp.sum(grouped, axis=0)
    client_part, span_part = side_by_side(
        (client_whole.astype(jnp.bfloat16), span_whole.astype(jnp.bfloat16)), "head", 1, 0
    )
    span_raw, bias_raw = (
        sum_by_parts(span_part.astype(jnp.bfloat16), CLIENT),
        sum_by_parts(bias_local.astype(jnp.bfloat16), CLIENT),
    )
    targets = lax.iota(jnp.int32, clients_here * lax.axis_size(CLIENT))
    selector = (targets[:, None] == client_ids[None, :]).astype(jnp.float32)
    embed_raw = sum_at_owner(
        jnp.dot(
            selector,
            client_part,
            precision=lax.Precision.HIGHEST,
            preferred_element_type=jnp.float32,
        ).astype(jnp.bfloat16),
        CLIENT,
        0,
    )
    leading = (lax.axis_index(CLIENT) == 0).astype(jnp.float32)
    small_square = leading * (jnp.sum(span_raw * span_raw) + jnp.sum(bias_raw * bias_raw))
    embed_square = jnp.sum(embed_raw * embed_raw)
    head_total, embed_total, small_total = in_one(
        (head_square, embed_square, small_square), (("client_0", "client_1"), ("client_2", "head"))
    )
    emit_total = emit_here * head_devices
    clients_total = clients_here * client_devices
    head_factor = clip_factor(head_total, hidden_width * emit_total)
    embed_factor = clip_factor(embed_total, clients_total * hidden_width)
    rest_factor = clip_factor(small_total, span_count * hidden_width + emit_total)
    return (
        head_factor * head_raw,
        rest_factor * bias_raw,
        embed_factor * embed_raw,
        rest_factor * span_raw,
    )


def solution(mesh):
    torus = Mesh(
        mesh.devices.reshape(4, 4, 2, mesh.shape["head"]),
        ("client_0", "client_1", "client_2", "head"),
    )
    return jax.shard_map(
        per_device,
        mesh=torus,
        in_specs=(P(CLIENT, None), P(CLIENT, "head"), P(None, "head"), P(CLIENT)),
        out_specs=(P(CLIENT, "head"), P("head"), P(CLIENT, "head"), P(None, "head")),
        check_vma=False,
    )
```

profile of v0, /device:TPU:1, one launch (start us, length us, event | category | flops | bytes accessed | tf_op | source)
XLA Modules:
  0.0 184.8 jit_solution(11156022891619115548)
XLA Ops:
  7.2 0.0 reduce-scatter.2.cloned.1.call-start
  7.2 18.3 %fusion.9 = bf16[4096,1024]{1,0:T(8,128)(2,1)} fusion(bf16[1280,4096]{1,0:T(8,128)(2,1)} %param.4, f32[1280,1024]{1,0:T(8,128)} %param.5), kind=kOutput, calls=%fused_computation.12 | convolution fusion | flops 10774380544 | bytes 24117248 | tf_op jit(solution)/shard_map/dot_general | solution.py:96
  25.5 0.0 slice-start
  25.5 0.0 reduce-scatter.2.cloned.1.call-update
  25.5 0.0 slice-start.1
  25.5 0.0 slice-start.2
  25.5 17.6 %convolution_convert_fusion = bf16[1280,4096]{1,0:T(8,128)(2,1)} fusion(bf16[4096,1024]{1,0:T(8,128)(2,1)} %param.6, f32[1280,1024]{1,0:T(8,128)} %param.5), kind=kOutput, calls=%fused_computation.10 | convolution fusion | flops 10743971840 | bytes 24117248 | tf_op jit(solution)/shard_map/dot_general | solution.py:105
  43.1 0.0 slice-done
  43.1 0.0 slice-done.1
  43.1 0.0 slice-done.2
  43.1 10.1 %fusion.6 = f32[1280,4096]{1,0:T(8,128)S(1)} fusion(bf16[1280,4096]{1,0:T(8,128)(2,1)S(1)} %bitcast.15, bf16[1280,4096]{1,0:T(8,128)(2,1)} %convolution_convert_fusion), kind=kLoop, calls=%fused_computation.9 | loop fusion | flops 52428800 | bytes 41943040 | tf_op jit(solution)/shard_map/mul | solution.py:109
  53.2 4.3 %fusion.19 = (bf16[16,4096]{1,0:T(8,128)(2,1)S(1)}, bf16[80,4096]{1,0:T(8,128)(2,1)S(1)}) fusion(f32[16,80,4096]{2,1,0:T(8,128)S(1)} %bitcast.13), kind=kLoop, calls=%fused_computation.35 | loop fusion | flops 10092544 | bytes 21757952 | tf_op jit(solution)/shard_map/reduce_sum | solution.py:111
  57.5 0.0 copy-start
  57.5 0.5 convert_element_type.88
  58.0 0.1 convert_element_type.86
  58.1 0.5 maximum_bitcast_fusion
  58.6 1.1 copy.27
  59.7 5.0 %all-to-all-start = ((bf16[4,96,1024]{2,1,0:T(8,128)(2,1)}), bf16[4,96,1024]{2,1,0:T(8,128)(2,1)S(1)}, u32[]{:S(2)}, u32[]{:S(2)}) async-start(bf16[4,96,1024]{2,1,0:T(8,128)(2,1)} %copy.27), calls=%async_computation.1 | async-start | bytes 1572864 | tf_op jit(solution)/shard_map/all_to_all | solution.py:20
  64.7 3.1 %reduce_sum.131 = bf16[1024]{0:T(1024)(128)(2,1)S(1)} reduce(f32[1280,1024]{1,0:T(8,128)} %param.5, f32[]{:T(128)} %constant.38.clone.1), dimensions={0}, to_apply=%region_9.10 | reduce | flops 1309696 | bytes 5244932 | tf_op jit(solution)/shard_map/reduce_sum | solution.py:104
  67.8 0.7 convert_element_type.96
  68.5 7.6 %all-to-all-done = bf16[4,96,1024]{2,1,0:T(8,128)(2,1)S(1)} async-done(((bf16[4,96,1024]{2,1,0:T(8,128)(2,1)}), bf16[4,96,1024]{2,1,0:T(8,128)(2,1)S(1)}, u32[]{:S(2)}, u32[]{:S(2)}) %all-to-all-start) | async-done | bytes 786464 | tf_op jit(solution)/shard_map/all_to_all | solution.py:20
  76.2 9.7 %all-to-all-start.4 = ((bf16[32,1,32]{2,1,0:T(2,128)(2,1)}), bf16[32,1,32]{2,1,0:T(2,128)(2,1)S(1)}, u32[]{:S(2)}, u32[]{:S(2)}) async-start(bf16[32,1,32]{2,1,0:T(2,128)(2,1)} %convert_element_type.96), calls=%async_computation.5 | async-start | bytes 32768 | tf_op jit(solution)/shard_map/all_to_all | solution.py:20
  85.9 0.1 convert_reduce_fusion.1
  86.1 0.1 all_to_all.41
  86.2 0.5 broadcast.22
  86.7 1.6 reduce.12
  88.3 0.7 reshape.119
  89.0 4.1 %all-to-all-done.4 = bf16[32,1,32]{2,1,0:T(2,128)(2,1)S(1)} async-done(((bf16[32,1,32]{2,1,0:T(2,128)(2,1)}), bf16[32,1,32]{2,1,0:T(2,128)(2,1)S(1)}, u32[]{:S(2)}, u32[]{:S(2)}) %all-to-all-start.4) | async-done | bytes 2080 | tf_op jit(solution)/shard_map/all_to_all | solution.py:20
  93.1 4.1 %all-to-all-start.2 = ((bf16[32,2,1280]{2,1,0:T(2,128)(2,1)}), bf16[32,2,1280]{2,1,0:T(2,128)(2,1)S(1)}, u32[]{:S(2)}, u32[]{:S(2)}) async-start(bf16[32,2,1280]{2,1,0:T(2,128)(2,1)} %reshape.119), calls=%async_computation.3 | async-start | bytes 327680 | tf_op jit(solution)/shard_map/all_to_all | solution.py:20
  97.2 0.1 reduce_sum.132
  97.2 8.0 %all-to-all-done.2 = bf16[32,2,1280]{2,1,0:T(2,128)(2,1)S(1)} async-done(((bf16[32,2,1280]{2,1,0:T(2,128)(2,1)}), bf16[32,2,1280]{2,1,0:T(2,128)(2,1)S(1)}, u32[]{:S(2)}, u32[]{:S(2)}) %all-to-all-start.2) | async-done | bytes 163872 | tf_op jit(solution)/shard_map/all_to_all | solution.py:20
  105.2 0.6 broadcast_in_dim.9
  105.8 3.8 %all-to-all-start.5 = ((bf16[32,1,32]{2,1,0:T(2,128)(2,1)}), bf16[32,1,32]{2,1,0:T(2,128)(2,1)S(1)}, u32[]{:S(2)}, u32[]{:S(2)}) async-start(bf16[32,1,32]{2,1,0:T(2,128)(2,1)} %broadcast_in_dim.9), calls=%async_computation.6 | async-start | bytes 32768 | tf_op jit(solution)/shard_map/all_to_all | solution.py:46
  109.7 0.1 reshape.120
  109.8 0.3 reduce_sum.129
  110.1 0.2 broadcast_in_dim.8
  110.3 1.6 reduce.13
  111.9 0.7 reshape.121
  112.6 4.1 %all-to-all-done.5 = bf16[32,1,32]{2,1,0:T(2,128)(2,1)S(1)} async-done(((bf16[32,1,32]{2,1,0:T(2,128)(2,1)}), bf16[32,1,32]{2,1,0:T(2,128)(2,1)S(1)}, u32[]{:S(2)}, u32[]{:S(2)}) %all-to-all-start.5) | async-done | bytes 2080 | tf_op jit(solution)/shard_map/all_to_all | solution.py:46
  116.6 4.2 %all-to-all-start.3 = ((bf16[32,2,1280]{2,1,0:T(2,128)(2,1)}), bf16[32,2,1280]{2,1,0:T(2,128)(2,1)S(1)}, u32[]{:S(2)}, u32[]{:S(2)}) async-start(bf16[32,2,1280]{2,1,0:T(2,128)(2,1)} %reshape.121), calls=%async_computation.4 | async-start | bytes 327680 | tf_op jit(solution)/shard_map/all_to_all | solution.py:46
  120.8 0.0 copy-done
  120.8 2.0 %convolution_convert_fusion.1 = bf16[512,1024]{1,0:T(8,128)(2,1)} fusion(s32[16]{0:T(128)S(1)} %copy-done, f32[96,1024]{1,0:T(8,128)S(1)} %convert_reduce_fusion.1), kind=kOutput, calls=%fused_computation.15 | convolution fusion | flops 101195776 | bytes 1114624 | tf_op jit(solution)/shard_map/dot_general | solution.py:123
  122.8 6.1 %all-to-all-done.3 = bf16[32,2,1280]{2,1,0:T(2,128)(2,1)S(1)} async-done(((bf16[32,2,1280]{2,1,0:T(2,128)(2,1)}), bf16[32,2,1280]{2,1,0:T(2,128)(2,1)S(1)}, u32[]{:S(2)}, u32[]{:S(2)}) %all-to-all-start.3) | async-done | bytes 163872 | tf_op jit(solution)/shard_map/all_to_all | solution.py:46
  128.9 3.9 %all-to-all-start.1 = ((bf16[32,16,1024]{2,1,0:T(8,128)(2,1)}), bf16[32,16,1024]{2,1,0:T(8,128)(2,1)S(1)}, u32[]{:S(2)}, u32[]{:S(2)}) async-start(bf16[32,16,1024]{2,1,0:T(8,128)(2,1)} %bitcast.3), calls=%async_computation.2 | async-start | bytes 2097152 | tf_op jit(solution)/shard_map/all_to_all | solution.py:20
  132.8 0.6 fusion.17
  133.4 0.1 reshape.122
  133.5 1.3 multiply_reduce_fusion.1
  136.1 13.8 %all-to-all-done.1 = bf16[32,16,1024]{2,1,0:T(8,128)(2,1)S(1)} async-done(((bf16[32,16,1024]{2,1,0:T(8,128)(2,1)}), bf16[32,16,1024]{2,1,0:T(8,128)(2,1)S(1)}, u32[]{:S(2)}, u32[]{:S(2)}) %all-to-all-start.1) | async-done | bytes 1048608 | tf_op jit(solution)/shard_map/all_to_all | solution.py:20
  149.9 0.2 convert_reduce_fusion
  150.1 0.6 multiply_reduce_fusion.2
  150.7 0.0 reduce-scatter.2.cloned.1.call-done
  150.7 1.7 fusion.14
  152.4 1.4 pad_maximum_fusion
  153.8 7.3 %all_to_all.50 = f32[8,1,3]{2,1,0:T(1,128)S(1)} all-to-all(f32[8,1,3]{2,1,0:T(1,128)S(1)} %broadcast_in_dim.10), channel_id=1, replica_groups=mesh['client_0'=4,'client_1'=4,'client_2'=2,'head'=4] {'client_2','head'}, dimensions={0} | all-to-all | bytes 192 | tf_op jit(solution)/shard_map/all_to_all | solution.py:46
  161.1 9.3 %all_to_all.51 = f32[16,1,3]{2,1,0:T(1,128)S(1)} all-to-all(f32[16,1,3]{2,1,0:T(1,128)S(1)} %broadcast_in_dim.11), channel_id=1, replica_groups=mesh['client_0'=4,'client_1'=4,'client_2'=2,'head'=4] {'client_0','clien..., dimensions={0} | all-to-all | bytes 384 | tf_op jit(solution)/shard_map/all_to_all | solution.py:46
  170.4 0.6 fusion.20
  171.7 0.9 multiply_reduce_fusion
  172.6 0.8 mul.88
  174.1 0.6 broadcast_multiply_fusion
  174.8 0.7 mul.83
  176.1 1.8 convert_multiply_fusion.2
  (7 shorter events, 0.1 us)
Async XLA Ops:
  7.2 143.5 %reduce-scatter.2.cloned.1.call-start = ((), (), s32[]{:S(2)}) async-start(), calls=%async_computation.9 | async-start | bytes 8650752 | tf_op jit(solution)/shard_map/reduce_scatter | solution.py:95
  25.5 17.6 %slice-start = ((s8[10485760]{0:T(1024)(128)(4,1)}), s8[2097152]{0:T(1024)(128)(4,1)S(1)}, s32[]{:S(2)}) async-start(s8[10485760]{0:T(1024)(128)(4,1)} %bitcast.14), calls=%async_computation.10 | async-start | bytes 4194304
  25.5 17.6 %slice-start.1 = ((s8[10485760]{0:T(1024)(128)(4,1)}), s8[4194304]{0:T(1024)(128)(4,1)S(1)}, s32[]{:S(2)}) async-start(s8[10485760]{0:T(1024)(128)(4,1)} %bitcast.14), calls=%async_computation.11 | async-start | bytes 8388608
  25.5 17.6 %slice-start.2 = ((s8[10485760]{0:T(1024)(128)(4,1)}), s8[4194304]{0:T(1024)(128)(4,1)S(1)}, s32[]{:S(2)}) async-start(s8[10485760]{0:T(1024)(128)(4,1)} %bitcast.14), calls=%async_computation.12 | async-start | bytes 8388608
  57.5 63.3 %copy-start = (s32[16]{0:T(128)S(1)}, s32[16]{0:T(128)}, u32[]{:S(2)}) copy-start(s32[16]{0:T(128)} %param.7) | copy-start | bytes 196
  59.7 16.4 %all-to-all-start = ((bf16[4,96,1024]{2,1,0:T(8,128)(2,1)}), bf16[4,96,1024]{2,1,0:T(8,128)(2,1)S(1)}, u32[]{:S(2)}, u32[]{:S(2)}) async-start(bf16[4,96,1024]{2,1,0:T(8,128)(2,1)} %copy.27), calls=%async_computation.1 | async-start | bytes 1572864 | tf_op jit(solution)/shard_map/all_to_all | solution.py:20
  76.2 16.9 %all-to-all-start.4 = ((bf16[32,1,32]{2,1,0:T(2,128)(2,1)}), bf16[32,1,32]{2,1,0:T(2,128)(2,1)S(1)}, u32[]{:S(2)}, u32[]{:S(2)}) async-start(bf16[32,1,32]{2,1,0:T(2,128)(2,1)} %convert_element_type.96), calls=%async_computation.5 | async-start | bytes 32768 | tf_op jit(solution)/shard_map/all_to_all | solution.py:20
  93.1 12.1 %all-to-all-start.2 = ((bf16[32,2,1280]{2,1,0:T(2,128)(2,1)}), bf16[32,2,1280]{2,1,0:T(2,128)(2,1)S(1)}, u32[]{:S(2)}, u32[]{:S(2)}) async-start(bf16[32,2,1280]{2,1,0:T(2,128)(2,1)} %reshape.119), calls=%async_computation.3 | async-start | bytes 327680 | tf_op jit(solution)/shard_map/all_to_all | solution.py:20
  105.8 10.8 %all-to-all-start.5 = ((bf16[32,1,32]{2,1,0:T(2,128)(2,1)}), bf16[32,1,32]{2,1,0:T(2,128)(2,1)S(1)}, u32[]{:S(2)}, u32[]{:S(2)}) async-start(bf16[32,1,32]{2,1,0:T(2,128)(2,1)} %broadcast_in_dim.9), calls=%async_computation.6 | async-start | bytes 32768 | tf_op jit(solution)/shard_map/all_to_all | solution.py:46
  116.6 12.2 %all-to-all-start.3 = ((bf16[32,2,1280]{2,1,0:T(2,128)(2,1)}), bf16[32,2,1280]{2,1,0:T(2,128)(2,1)S(1)}, u32[]{:S(2)}, u32[]{:S(2)}) async-start(bf16[32,2,1280]{2,1,0:T(2,128)(2,1)} %reshape.121), calls=%async_computation.4 | async-start | bytes 327680 | tf_op jit(solution)/shard_map/all_to_all | solution.py:46
  128.9 21.1 %all-to-all-start.1 = ((bf16[32,16,1024]{2,1,0:T(8,128)(2,1)}), bf16[32,16,1024]{2,1,0:T(8,128)(2,1)S(1)}, u32[]{:S(2)}, u32[]{:S(2)}) async-start(bf16[32,16,1024]{2,1,0:T(8,128)(2,1)} %bitcast.3), calls=%async_computation.2 | async-start | bytes 2097152 | tf_op jit(solution)/shard_map/all_to_all | solution.py:20
Sparse Core Ops, SparseCore 0:
  25.6 95.5 reduce-scatter.1
where the time goes:
time: 186 us; the launch traced here: 185 us
  waiting for transfers between devices  43.7 us (23%)
  matrix products  37.8 us (20%)
  starting transfers between devices  30.8 us (17%)
  other arithmetic  30.8 us (17%)
  between operations  17.6 us (9%)
  blocking collectives  16.6 us (9%)
  local copies, waits for them, and re-layouts  7.57 us (4%)
    all_to_all x4, waiting for transfers between devices, sum_at_owner(): lax.all_to_all(tiles, axis, split_axis=0, concat_axis=0, tiled=True)  33.5 us
    all_to_all x4, starting transfers between devices, sum_at_owner(): lax.all_to_all(tiles, axis, split_axis=0, concat_axis=0, tiled=True)  22.8 us
    dot_general x1, matrix products, per_device(): lax.dot_general(hidden, delta_low, (((0,), (0,)), ((), ())), preferred_el...  18.3 us
    dot_general x1, matrix products, per_device(): lax.dot_general(delta_low, head_weight, (((1,), (1,)), ((), ())), preferr...  17.6 us
    all_to_all x2, blocking collectives, sent_to_all(): lax.all_to_all(jnp.broadcast_to(x[None], (peers, *x.shape)), axis, 0, 0,...  16.6 us
    all_to_all x2, waiting for transfers between devices, sent_to_all(): lax.all_to_all(jnp.broadcast_to(x[None], (peers, *x.shape)), axis, 0, 0,...  10.2 us
    mul x1, other arithmetic, per_device(): rounded.astype(jnp.float32) * silu_slope(pre.astype(jnp.float32))  10.1 us
    all_to_all x2, starting transfers between devices, sent_to_all(): lax.all_to_all(jnp.broadcast_to(x[None], (peers, *x.shape)), axis, 0, 0,...  7.99 us
  transfers between devices with their start and end apart: 7, of which 6 were waited for; matrix products, arithmetic and copies ran while one was open for 27% of the time, Pallas kernels for 0%

commit v1 on v0

--- a/solution.py
+++ b/solution.py
@@ -1,13 +1,26 @@
+import functools
+
 import jax
 import jax.numpy as jnp
 from jax import lax
+from jax.experimental import pallas as pl
+from jax.experimental.pallas import tpu as pltpu
 from jax.sharding import Mesh
 from jax.sharding import PartitionSpec as P
 
 CLIENT = ("client_0", "client_1", "client_2")
-
-
 EPSILON = 1e-06
+MESH = pl.DeviceIdType.MESH
+
+ORDER = ((2, 2), (2, 1), (2, 3), (2, 0), (1, 2), (3, 2), (0, 2), (1, 1), (3, 1), (0, 1), (1, 3), (3, 3), (0, 3), (1, 0), (3, 0), (0, 0))
+STEPS = 16
+BLOCK = 256
+LANES = 128
+YORDER = (2, 1, 3, 0)
+
+
+def digits(values):
+    return sum(v * 4**i for i, v in enumerate(values))
 
 
 def cut_along(x, dim, peers):
@@ -19,15 +32,6 @@
     tiles = cut_along(x, dim, lax.axis_size(axis))
     arrived = lax.all_to_all(tiles, axis, split_axis=0, concat_axis=0, tiled=True)
     return arrived.astype(jnp.float32).sum(axis=0)
-
-
-def side_by_side(arrays, axis, dim, along):
-    ends, at = ([], 0)
-    for a in arrays[:-1]:
-        at += a.shape[along]
-        ends.append(at)
-    both = jnp.concatenate(arrays, axis=along)
-    return tuple(jnp.split(sum_at_owner(both, axis, dim), ends, axis=along))
 
 
 def padded_to(lines, peers):
@@ -74,13 +78,391 @@
     return tuple((subtotal[b:e].reshape(a.shape) for a, b, e in zip(arrays, ends, ends[1:])))
 
 
-def silu_slope(values):
-    sigma = jax.nn.sigmoid(values)
-    return sigma * (1.0 + values * (1.0 - sigma))
-
-
 def clip_factor(total, number):
     return jnp.minimum(1.0, 1.0 / jnp.sqrt(total / number + EPSILON))
+
+
+def kernel(
+    pre_hbm, delta_hbm, weight_hbm, head_out, sums_out, bias_out,
+    stage, low, low_t, weight, pre_b, hid_a, hid_b, slope, prod, crecv, acc_a, acc_b, sums, sums_low, yrecv, r_a, r_b, r_a2, r_b2,
+    delta_sem, weight_sem, pre_sem, c_send, c_recv, a_send, a_recv, b_send, b_recv, a2_send, a2_recv, b2_send, b2_recv, y_send, y_recv,
+):
+    rows = low.shape[0]
+    clients = 16
+    spans = rows // clients
+    half = prod.shape[2] // 2
+    z, x, c, y = (lax.axis_index(a) for a in (*CLIENT, "head"))
+
+    def ring(one, offset):
+        along_z = one * (1 - c) + (1 - one) * c
+        return lax.rem(z + offset * along_z, 4), lax.rem(x + offset * (1 - along_z), 4), c, y
+
+    partner = (z, x, 1 - c, y)
+    barrier = pltpu.get_barrier_semaphore()
+    others = [partner] + [ring(one, offset) for one in (1, 0) for offset in (1, 3)]
+    others += [(z, x, c, lax.rem(y + offset, 4)) for offset in (1, 2, 3)]
+    for other in others:
+        pl.semaphore_signal(barrier, inc=1, device_id=other, device_id_type=MESH)
+
+    def delta_copy(block):
+        slot = block % 3
+        return pltpu.make_async_copy(delta_hbm.at[pl.ds(block * 256, 256), :], stage.at[slot], delta_sem.at[slot])
+
+    def chips(dp, dq):
+        first = lax.rem(z + dp, 4) * 4 + lax.rem(x + dq, 4)
+        second = lax.rem(z + dq, 4) * 4 + lax.rem(x + dp, 4)
+        return first, second
+
+    def pre_copies(dp, dq, slot):
+        out = []
+        for h, chip in enumerate(chips(dp, dq)):
+            column = pl.multiple_of((chip * 2 + h) * LANES, LANES)
+            out.append(
+                pltpu.make_async_copy(
+                    pre_hbm.at[:, pl.ds(column, LANES)],
+                    pre_b.at[slot, :, pl.ds(h * LANES, LANES)],
+                    pre_sem.at[slot, h],
+                )
+            )
+        return out
+
+    def weight_copy(part):
+        size = weight.shape[0] // 4
+        return pltpu.make_async_copy(weight_hbm.at[pl.ds(part * size, size), :], weight.at[pl.ds(part * size, size), :], weight_sem.at[part])
+
+    def silu_to(slot, hid, at):
+        for b in range(rows // 32):
+            lines = pl.ds(b * 32, 32)
+            v = pre_b[slot, lines, :].astype(jnp.float32)
+            gate = 1.0 / (1.0 + jnp.exp(-v))
+            value = v * gate
+            hid[lines, :] = value.astype(jnp.bfloat16)
+            slant = (gate + value * (1.0 - gate)).astype(jnp.bfloat16)
+            for h in range(2):
+                slope[at[h], lines, pl.ds(h * LANES, LANES)] = slant[:, h * LANES : (h + 1) * LANES]
+
+    def remote(src, dst, send, recv, to):
+        return pltpu.make_async_remote_copy(src_ref=src, dst_ref=dst, send_sem=send, recv_sem=recv, device_id=to, device_id_type=MESH)
+
+    lower, upper = pl.ds(0, half), pl.ds(half, half)
+
+    def core_copy(s):
+        return remote(prod.at[s, 1 - c], crecv.at[s], c_send.at[s], c_recv.at[s], partner)
+
+    def a_copies(i):
+        return (
+            remote(prod.at[i, c, lower], r_a.at[i, 0], a_send.at[i, 0], a_recv.at[i, 0], ring(1, 3)),
+            remote(prod.at[i, c, upper], r_a.at[i, 1], a_send.at[i, 1], a_recv.at[i, 1], ring(1, 1)),
+        )
+
+    def b_copies(i):
+        ahead, behind = 4 + 3 * i, 5 + 3 * i
+
+        def one(chunk, part, side, k, to):
+            return remote(prod.at[chunk, c, part], r_b.at[i, side, part], b_send.at[i, k], b_recv.at[i, k], to)
+
+        return (
+            one(ahead, lower, 0, 0, ring(1, 1)),
+            one(behind, upper, 1, 1, ring(1, 3)),
+            one(ahead, upper, 0, 2, ring(1, 1)),
+            one(behind, lower, 1, 3, ring(1, 3)),
+        )
+
+    def a2_copies():
+        chunk = 6
+        return (
+            remote(prod.at[chunk, c, lower], r_a2.at[0], a2_send.at[0], a2_recv.at[0], ring(0, 3)),
+            remote(prod.at[chunk, c, upper], r_a2.at[1], a2_send.at[1], a2_recv.at[1], ring(0, 1)),
+        )
+
+    def b2_copies():
+        def one(chunk, part, side, k, to):
+            return remote(prod.at[chunk, c, part], r_b2.at[side, part], b2_send.at[k], b2_recv.at[k], to)
+
+        return (
+            one(9, lower, 0, 0, ring(0, 1)),
+            one(12, upper, 1, 1, ring(0, 3)),
+            one(9, upper, 0, 2, ring(0, 1)),
+            one(12, lower, 1, 3, ring(0, 3)),
+        )
+
+    def core_add(s):
+        core_copy(s).wait_recv()
+        prod[s, c] = prod[s, c] + crecv[s]
+
+    def do_a(i):
+        for copy in a_copies(i):
+            copy.start()
+
+    def do_b(i):
+        first, second, third, fourth = b_copies(i)
+        first.start()
+        second.start()
+        from_plus, from_minus = a_copies(i)
+        ahead, behind = 4 + 3 * i, 5 + 3 * i
+        from_minus.wait_recv()
+        prod[ahead, c, upper] = prod[ahead, c, upper] + r_a[i, 1]
+        from_plus.wait_recv()
+        prod[behind, c, lower] = prod[behind, c, lower] + r_a[i, 0]
+        third.start()
+        fourth.start()
+
+    def three(a, b, d):
+        return a.astype(jnp.float32) + b.astype(jnp.float32) + d.astype(jnp.float32)
+
+    def do_f(i):
+        for copy in b_copies(i):
+            copy.wait_recv()
+        chunk = 6 + 3 * i
+        prod[chunk, c] = three(prod[chunk, c], r_b[i, 0], r_b[i, 1]).astype(jnp.bfloat16)
+
+    def do_a2():
+        for copy in a2_copies():
+            copy.start()
+
+    def do_b2():
+        first, second, third, fourth = b2_copies()
+        first.start()
+        second.start()
+        from_plus, from_minus = a2_copies()
+        from_minus.wait_recv()
+        prod[9, c, upper] = prod[9, c, upper] + r_a2[1]
+        from_plus.wait_recv()
+        prod[12, c, lower] = prod[12, c, lower] + r_a2[0]
+        third.start()
+        fourth.start()
+
+    def do_final():
+        for copy in b2_copies():
+            copy.wait_recv()
+        whole = three(prod[15, c], r_b2[0], r_b2[1])
+        head_out[...] = whole.T
+
+    def y_copy(group):
+        to = lax.rem(y + jnp.int32(0) + offset_of(group), 4)
+        return remote(
+            sums_low.at[pl.ds(4 * group, 4)], yrecv.at[group], y_send.at[group], y_recv.at[group], (z, x, c, to)
+        )
+
+    def offset_of(group):
+        return YORDER[group]
+
+    for block in range(3):
+        delta_copy(block).start()
+    for s in range(4):
+        for copy in pre_copies(*ORDER[s], s):
+            copy.start()
+    bias = jnp.zeros((1, low.shape[1]), jnp.float32)
+    for block in range(rows // 256):
+        delta_copy(block).wait()
+        lines = pl.ds(block * 256, 256)
+        values = stage[block % 3]
+        bias = bias + jnp.sum(values, axis=0, keepdims=True)
+        rounded = values.astype(jnp.bfloat16)
+        low[lines, :] = rounded
+        low_t[:, lines] = rounded.T
+        if block + 3 < rows // 256:
+            delta_copy(block + 3).start()
+    bias_out[...] = bias
+    for part in range(4):
+        weight_copy(part).start()
+    for copy in pre_copies(*ORDER[0], 0):
+        copy.wait()
+    silu_to(0, hid_a, chips(*ORDER[0]))
+    for copy in pre_copies(*ORDER[4], 0):
+        copy.start()
+    pl.semaphore_wait(barrier, len(others))
+
+    next_p, next_q = digits([o[0] for o in ORDER[1:]]), digits([o[1] for o in ORDER[1:]])
+    load_p, load_q = digits([o[0] for o in ORDER[5:]]), digits([o[1] for o in ORDER[5:]])
+
+    def first_product(i, carry):
+        np_, nq_, lp_, lq_ = carry
+        for k, (now, later) in enumerate(((hid_a, hid_b), (hid_b, hid_a))):
+            s = 2 * i + k
+            slot = lax.rem(s + 1, 4)
+            dp, dq = lax.rem(np_, 4), lax.rem(nq_, 4)
+
+            @pl.when(s < STEPS - 1)
+            def _():
+                for copy in pre_copies(dp, dq, slot):
+                    copy.wait()
+
+            last = lax.div(s, STEPS - 1)
+            at = [chip * (1 - last) + STEPS * last for chip in chips(dp, dq)]
+            silu_to(slot, later, at)
+            product = jnp.dot(low_t[...], now[...], preferred_element_type=jnp.float32).astype(jnp.bfloat16)
+            for h in range(2):
+                prod[s, h] = product[:, h * LANES : (h + 1) * LANES]
+
+            @pl.when(s + 5 < STEPS)
+            def _():
+                for copy in pre_copies(lax.rem(lp_, 4), lax.rem(lq_, 4), slot):
+                    copy.start()
+
+            core_copy(s).start()
+
+            @pl.when(s >= 2)
+            def _():
+                core_add(s - 2)
+
+            if k == 0:
+                pl.when(i == 1)(lambda: do_a(0))
+                pl.when(i == 2)(lambda: do_a(2))
+                pl.when(i == 5)(lambda: do_b(1))
+            else:
+                pl.when(i == 1)(lambda: do_a(1))
+                pl.when(i == 2)(lambda: do_a(3))
+                pl.when(i == 3)(lambda: do_b(0))
+                pl.when(i == 6)(lambda: do_b(2))
+
+                @pl.when(i == 7)
+                def _():
+                    do_f(0)
+                    do_a2()
+
+            np_, nq_, lp_, lq_ = (lax.div(t, 4) for t in (np_, nq_, lp_, lq_))
+        return np_, nq_, lp_, lq_
+
+    lax.fori_loop(0, STEPS // 2, first_product, tuple(jnp.int32(t) for t in (next_p, next_q, load_p, load_q)))
+
+    def reduce_rows(acc, chunk, u):
+        span = jnp.zeros((spans, BLOCK), jnp.float32)
+        for client in range(clients):
+            lines = pl.ds(client * spans, spans)
+            grad = acc[lines, :] * slope[chunk, lines, :].astype(jnp.float32)
+            span = span + grad
+            whole = jnp.sum(grad, axis=0, keepdims=True)
+            sums[u, pl.ds(spans + client, 1), :] = whole
+        sums[u, pl.ds(0, spans), :] = span
+        sums_low[u] = sums[u].astype(jnp.bfloat16)
+
+    for part in range(4):
+        weight_copy(part).wait()
+
+    def second_product(g, carry):
+        before, table = carry
+        chunk0 = lax.rem(y + lax.rem(table, 4), 4) * 4
+        for t in range(4):
+            u = 4 * g + t
+            now, last = (acc_a, acc_b) if t % 2 == 0 else (acc_b, acc_a)
+            chunk = chunk0 + t
+            previous = before if t == 0 else chunk - 1
+            slot = lax.rem(u + STEPS, STEPS + 1)
+            reduce_rows(last, previous, slot)
+            lines = pl.ds(pl.multiple_of(chunk * BLOCK, BLOCK), BLOCK)
+            now[...] = lax.dot_general(low[...], weight[lines, :], (((1,), (1,)), ((), ())), preferred_element_type=jnp.float32)
+            if t == 0:
+
+                @pl.when(g == 0)
+                def _():
+                    core_add(STEPS - 2)
+                    do_b(3)
+
+                @pl.when(g == 3)
+                def _():
+                    do_final()
+
+                for group in range(3):
+                    pl.when(g == group + 1)(lambda group=group: y_copy(group).start())
+            elif t == 1:
+
+                @pl.when(g == 0)
+                def _():
+                    core_add(STEPS - 1)
+
+            elif t == 2:
+
+                pl.when(g == 0)(lambda: do_f(1))
+
+                @pl.when(g == 1)
+                def _():
+                    do_f(2)
+                    do_b2()
+
+                pl.when(g == 2)(lambda: do_f(3))
+        return chunk0 + 3, lax.div(table, 4)
+
+    final_chunk, _ = lax.fori_loop(0, 4, second_product, (jnp.int32(0), jnp.int32(digits(YORDER))))
+    reduce_rows(acc_b, final_chunk, STEPS - 1)
+    for group in range(3):
+        y_copy(group).wait_recv()
+    for t in range(4):
+        total = sums[12 + t]
+        for group in range(3):
+            total = total + yrecv[group, t].astype(jnp.float32)
+        sums_out[:, pl.ds(t * BLOCK, BLOCK)] = total
+
+    def all_sent(s, _):
+        core_copy(s).wait_send()
+        return 0
+
+    lax.fori_loop(0, STEPS, all_sent, 0)
+    for i in range(4):
+        for copy in (*a_copies(i), *b_copies(i)):
+            copy.wait_send()
+    for copy in (*a2_copies(), *b2_copies()):
+        copy.wait_send()
+    for group in range(3):
+        y_copy(group).wait_send()
+
+
+def local_products(pre, delta, head_weight):
+    rows, width = pre.shape
+    here = delta.shape[1]
+    bf16, f32 = jnp.bfloat16, jnp.float32
+    dma = pltpu.SemaphoreType.DMA
+    spans = rows // 16
+    anywhere = pl.BlockSpec(memory_space=pl.ANY)
+    in_vmem = pl.BlockSpec(memory_space=pltpu.VMEM)
+    return pl.pallas_call(
+        kernel,
+        name="products",
+        out_shape=(
+            jax.ShapeDtypeStruct((LANES, here), f32),
+            jax.ShapeDtypeStruct((spans + 16, here), f32),
+            jax.ShapeDtypeStruct((1, here), f32),
+        ),
+        in_specs=[anywhere] * 3,
+        out_specs=[in_vmem] * 3,
+        scratch_shapes=[
+            pltpu.VMEM((3, 256, here), f32),
+            pltpu.VMEM((rows, here), bf16),
+            pltpu.VMEM((here, rows), bf16),
+            pltpu.VMEM((width, here), bf16),
+            pltpu.VMEM((4, rows, BLOCK), bf16),
+            pltpu.VMEM((rows, BLOCK), bf16),
+            pltpu.VMEM((rows, BLOCK), bf16),
+            pltpu.VMEM((STEPS + 1, rows, BLOCK), bf16),
+            pltpu.VMEM((STEPS, 2, here, LANES), bf16),
+            pltpu.VMEM((STEPS, here, LANES), bf16),
+            pltpu.VMEM((rows, BLOCK), f32),
+            pltpu.VMEM((rows, BLOCK), f32),
+            pltpu.VMEM((STEPS + 1, spans + 16, BLOCK), f32),
+            pltpu.VMEM((STEPS + 1, spans + 16, BLOCK), bf16),
+            pltpu.VMEM((3, 4, spans + 16, BLOCK), bf16),
+            pltpu.VMEM((4, 2, here // 2, LANES), bf16),
+            pltpu.VMEM((4, 2, here, LANES), bf16),
+            pltpu.VMEM((2, here // 2, LANES), bf16),
+            pltpu.VMEM((2, here, LANES), bf16),
+            dma((3,)),
+            dma((4,)),
+            dma((4, 2)),
+            dma((STEPS,)),
+            dma((STEPS,)),
+            dma((4, 2)),
+            dma((4, 2)),
+            dma((4, 4)),
+            dma((4, 4)),
+            dma((2,)),
+            dma((2,)),
+            dma((4,)),
+            dma((4,)),
+            dma((3,)),
+            dma((3,)),
+        ],
+        compiler_params=pltpu.CompilerParams(collective_id=0, has_side_effects=True, vmem_limit_bytes=67_000_000),
+    )(pre, delta, head_weight)
 
 
 def per_device(pre, delta, head_weight, client_ids):
@@ -90,29 +472,9 @@
     span_count = rows_here // clients_here
     head_devices = lax.axis_size("head")
     client_devices = lax.axis_size(CLIENT)
-    hidden = jax.nn.silu(pre.astype(jnp.float32)).astype(jnp.bfloat16)
-    delta_low = delta.astype(jnp.bfloat16)
-    head_raw = lax.psum_scatter(
-        lax.dot_general(
-            hidden, delta_low, (((0,), (0,)), ((), ())), preferred_element_type=jnp.float32
-        ).astype(jnp.bfloat16),
-        CLIENT,
-        scatter_dimension=0,
-        tiled=True,
-    ).astype(jnp.float32)
+    head_raw, sums, bias = local_products(pre, delta, head_weight)
     head_square = jnp.sum(head_raw * head_raw)
-    bias_local = jnp.sum(delta, axis=0)
-    partial_sum = lax.dot_general(
-        delta_low, head_weight, (((1,), (1,)), ((), ())), preferred_element_type=jnp.float32
-    )
-    rounded = lax.optimization_barrier(partial_sum.astype(jnp.bfloat16))
-    block_grad = rounded.astype(jnp.float32) * silu_slope(pre.astype(jnp.float32))
-    grouped = block_grad.reshape(clients_here, span_count, hidden_width)
-    client_whole = jnp.sum(grouped, axis=1)
-    span_whole = jnp.sum(grouped, axis=0)
-    client_part, span_part = side_by_side(
-        (client_whole.astype(jnp.bfloat16), span_whole.astype(jnp.bfloat16)), "head", 1, 0
-    )
+    span_part, client_part, bias_local = sums[:span_count], sums[span_count:], bias[0]
     span_raw, bias_raw = (
         sum_by_parts(span_part.astype(jnp.bfloat16), CLIENT),
         sum_by_parts(bias_local.astype(jnp.bfloat16), CLIENT),

time: 186 us -> 173 us (0.930)
  Pallas kernels: 0 us -> 69.3 us
  matrix products: 37.8 us -> 2.79 us
  other arithmetic: 30.8 us -> 11.5 us
  between operations: 17.6 us -> 4.18 us
  waiting for transfers between devices: 43.7 us -> 33.2 us
  starting transfers between devices: 30.8 us -> 25.5 us
    pallas_call x0 -> x1, Pallas kernels: none -> 69.3 us  [local_products(): pl.pallas_call(kernel, name='products', out_shape=(jax.ShapeDtypeStruct((...]
    dot_general x2 -> x0, matrix products: 35.8 us -> none  [the longest x1 18.3 us: per_device(): lax.dot_general(hidden, delta_low, (((0,), (0,)), ((), ())), preferred_el...]
    mul x1 -> x0, other arithmetic: 10.1 us -> none  [per_device(): rounded.astype(jnp.float32) * silu_slope(pre.astype(jnp.float32))]
    all_to_all x4 -> x3, waiting for transfers between devices: 33.5 us -> 23.9 us  [sum_at_owner(): lax.all_to_all(tiles, axis, split_axis=0, concat_axis=0, tiled=True)]
    reduce_sum x2 -> x0, other arithmetic: 7.43 us -> none  [the longest x1 4.32 us: per_device(): client_whole = jnp.sum(grouped, axis=1)]
    all_to_all x4 -> x3, starting transfers between devices: 22.8 us -> 17.5 us  [sum_at_owner(): lax.all_to_all(tiles, axis, split_axis=0, concat_axis=0, tiled=True)]
  transfers between devices with their start and end apart: 7 -> 5, of which waited for: 6 -> 5; matrix products, arithmetic and copies ran while one was open for 27% -> 7% of each run, Pallas kernels for 0% -> 0%
where the time goes in v1:
time: 173 us; the launch traced here: 172 us
  Pallas kernels  69.3 us (40%)
  waiting for transfers between devices  33.2 us (19%)
  starting transfers between devices  25.5 us (15%)
  blocking collectives  18.2 us (11%)
  other arithmetic  11.5 us (7%)
  local copies, waits for them, and re-layouts  6.86 us (4%)
  between operations  4.18 us (2%)
  matrix products  2.79 us (2%)
    pallas_call x1, Pallas kernels, local_products(): pl.pallas_call(kernel, name='products', out_shape=(jax.ShapeDtypeStruct((...  69.3 us
    all_to_all x3, waiting for transfers between devices, sum_at_owner(): lax.all_to_all(tiles, axis, split_axis=0, concat_axis=0, tiled=True)  23.9 us
    all_to_all x2, blocking collectives, sent_to_all(): lax.all_to_all(jnp.broadcast_to(x[None], (peers, *x.shape)), axis, 0, 0,...  18.2 us
    all_to_all x3, starting transfers between devices, sum_at_owner(): lax.all_to_all(tiles, axis, split_axis=0, concat_axis=0, tiled=True)  17.5 us
    all_to_all x2, waiting for transfers between devices, sent_to_all(): lax.all_to_all(jnp.broadcast_to(x[None], (peers, *x.shape)), axis, 0, 0,...  9.31 us
    all_to_all x2, starting transfers between devices, sent_to_all(): lax.all_to_all(jnp.broadcast_to(x[None], (peers, *x.shape)), axis, 0, 0,...  7.99 us
  transfers between devices with their start and end apart: 5, of which 5 were waited for; matrix products, arithmetic and copies ran while one was open for 7% of the time, Pallas kernels for 0%

profile of v1, /device:TPU:1, one launch (start us, length us, event | category | flops | bytes accessed | tf_op | source)
XLA Modules:
  0.0 171.6 jit_solution(13647980707404309108)
XLA Ops:
  0.6 0.0 copy-start.1
  0.6 69.3 %products.1 = (f32[128,1024]{1,0:T(8,128)}, f32[96,1024]{1,0:T(8,128)}, f32[1,1024]{1,0:T(1,128)}) custom-call(bf16[1280,4096]{1,0:T(8,128)(2,1)} %pre_hbm.1, f32[1280,1024]{1,0:T(8,128)} %delta_hbm.1, bf16[4096,1024]{1,0:T(8,128)(2,1)} %weight_hbm.1), custom_call_target="tpu_custom_call" | custom-call | tf_op jit(solution)/shard_map/products/pallas_call | solution.py:418
  70.0 0.0 copy-start
  70.0 0.8 convert_reduce_fusion.1
  70.8 0.7 convert_element_type.45
  71.5 9.2 %all-to-all-start.3 = ((bf16[32,1,32]{2,1,0:T(2,128)(2,1)}), bf16[32,1,32]{2,1,0:T(2,128)(2,1)S(1)}, u32[]{:S(2)}, u32[]{:S(2)}) async-start(bf16[32,1,32]{2,1,0:T(2,128)(2,1)} %convert_element_type.45), calls=%async_computation.3 | async-start | bytes 32768 | tf_op jit(solution)/shard_map/all_to_all | solution.py:33
  80.6 1.0 slice.25
  81.6 0.1 all_to_all.37
  81.8 0.5 broadcast.20
  82.3 1.6 reduce.14
  83.9 0.7 reshape.109
  84.6 2.9 %all-to-all-done.3 = bf16[32,1,32]{2,1,0:T(2,128)(2,1)S(1)} async-done(((bf16[32,1,32]{2,1,0:T(2,128)(2,1)}), bf16[32,1,32]{2,1,0:T(2,128)(2,1)S(1)}, u32[]{:S(2)}, u32[]{:S(2)}) %all-to-all-start.3) | async-done | bytes 2080 | tf_op jit(solution)/shard_map/all_to_all | solution.py:33
  87.5 4.4 %all-to-all-start.1 = ((bf16[32,2,1280]{2,1,0:T(2,128)(2,1)}), bf16[32,2,1280]{2,1,0:T(2,128)(2,1)S(1)}, u32[]{:S(2)}, u32[]{:S(2)}) async-start(bf16[32,2,1280]{2,1,0:T(2,128)(2,1)} %reshape.109), calls=%async_computation.1 | async-start | bytes 327680 | tf_op jit(solution)/shard_map/all_to_all | solution.py:33
  92.0 0.1 reduce_sum.92
  92.0 7.9 %all-to-all-done.1 = bf16[32,2,1280]{2,1,0:T(2,128)(2,1)S(1)} async-done(((bf16[32,2,1280]{2,1,0:T(2,128)(2,1)}), bf16[32,2,1280]{2,1,0:T(2,128)(2,1)S(1)}, u32[]{:S(2)}, u32[]{:S(2)}) %all-to-all-start.1) | async-done | bytes 163872 | tf_op jit(solution)/shard_map/all_to_all | solution.py:33
  99.9 0.6 broadcast_in_dim.9
  100.5 3.8 %all-to-all-start.4 = ((bf16[32,1,32]{2,1,0:T(2,128)(2,1)}), bf16[32,1,32]{2,1,0:T(2,128)(2,1)S(1)}, u32[]{:S(2)}, u32[]{:S(2)}) async-start(bf16[32,1,32]{2,1,0:T(2,128)(2,1)} %broadcast_in_dim.9), calls=%async_computation.4 | async-start | bytes 32768 | tf_op jit(solution)/shard_map/all_to_all | solution.py:50
  104.3 0.1 reshape.110
  104.5 0.3 reduce_sum.90
  104.8 0.2 broadcast_in_dim.8
  104.9 1.6 reduce.15
  106.5 0.7 reshape.111
  107.2 4.1 %all-to-all-done.4 = bf16[32,1,32]{2,1,0:T(2,128)(2,1)S(1)} async-done(((bf16[32,1,32]{2,1,0:T(2,128)(2,1)}), bf16[32,1,32]{2,1,0:T(2,128)(2,1)S(1)}, u32[]{:S(2)}, u32[]{:S(2)}) %all-to-all-start.4) | async-done | bytes 2080 | tf_op jit(solution)/shard_map/all_to_all | solution.py:50
  111.3 4.2 %all-to-all-start.2 = ((bf16[32,2,1280]{2,1,0:T(2,128)(2,1)}), bf16[32,2,1280]{2,1,0:T(2,128)(2,1)S(1)}, u32[]{:S(2)}, u32[]{:S(2)}) async-start(bf16[32,2,1280]{2,1,0:T(2,128)(2,1)} %reshape.111), calls=%async_computation.2 | async-start | bytes 327680 | tf_op jit(solution)/shard_map/all_to_all | solution.py:50
  115.5 0.0 copy-done.1
  115.5 2.8 %convolution_convert_fusion = bf16[512,1024]{1,0:T(8,128)(2,1)} fusion(s32[16]{0:T(128)S(1)} %copy-done.1, f32[96,1024]{1,0:T(8,128)} %get-tuple-element.8), kind=kOutput, calls=%fused_computation.1 | convolution fusion | flops 101195776 | bytes 1114176 | tf_op jit(solution)/shard_map/dot_general | solution.py:485
  118.3 5.2 %all-to-all-done.2 = bf16[32,2,1280]{2,1,0:T(2,128)(2,1)S(1)} async-done(((bf16[32,2,1280]{2,1,0:T(2,128)(2,1)}), bf16[32,2,1280]{2,1,0:T(2,128)(2,1)S(1)}, u32[]{:S(2)}, u32[]{:S(2)}) %all-to-all-start.2) | async-done | bytes 163872 | tf_op jit(solution)/shard_map/all_to_all | solution.py:50
  123.5 3.9 %all-to-all-start = ((bf16[32,16,1024]{2,1,0:T(8,128)(2,1)}), bf16[32,16,1024]{2,1,0:T(8,128)(2,1)S(1)}, u32[]{:S(2)}, u32[]{:S(2)}) async-start(bf16[32,16,1024]{2,1,0:T(8,128)(2,1)} %bitcast.1), calls=%async_computation | async-start | bytes 2097152 | tf_op jit(solution)/shard_map/all_to_all | solution.py:33
  127.5 0.0 copy-done
  127.5 0.7 multiply_reduce_fusion
  128.2 0.6 fusion.2
  128.8 0.1 reshape.112
  128.9 1.3 multiply_reduce_fusion.2
  131.5 13.1 %all-to-all-done = bf16[32,16,1024]{2,1,0:T(8,128)(2,1)S(1)} async-done(((bf16[32,16,1024]{2,1,0:T(8,128)(2,1)}), bf16[32,16,1024]{2,1,0:T(8,128)(2,1)S(1)}, u32[]{:S(2)}, u32[]{:S(2)}) %all-to-all-start) | async-done | bytes 1048608 | tf_op jit(solution)/shard_map/all_to_all | solution.py:33
  144.6 0.2 convert_reduce_fusion
  144.8 0.6 multiply_reduce_fusion.3
  145.4 1.4 pad_maximum_fusion
  146.8 9.0 %all_to_all.45 = f32[8,1,3]{2,1,0:T(1,128)S(1)} all-to-all(f32[8,1,3]{2,1,0:T(1,128)S(1)} %broadcast_in_dim.10), channel_id=1, replica_groups=mesh['client_0'=4,'client_1'=4,'client_2'=2,'head'=4] {'client_2','head'}, dimensions={0} | all-to-all | bytes 192 | tf_op jit(solution)/shard_map/all_to_all | solution.py:50
  155.7 9.3 %all_to_all.46 = f32[16,1,3]{2,1,0:T(1,128)S(1)} all-to-all(f32[16,1,3]{2,1,0:T(1,128)S(1)} %broadcast_in_dim.11), channel_id=1, replica_groups=mesh['client_0'=4,'client_1'=4,'client_2'=2,'head'=4] {'client_0','clien..., dimensions={0} | all-to-all | bytes 384 | tf_op jit(solution)/shard_map/all_to_all | solution.py:50
  165.1 0.6 fusion.3
  166.3 0.8 broadcast_multiply_fusion
  167.9 0.9 multiply_reduce_fusion.1
  168.8 0.7 mul.66
  170.2 0.6 broadcast_multiply_fusion.1
  170.8 0.8 mul.71
  (5 shorter events, 0.1 us)
Async XLA Ops:
  0.6 114.9 %copy-start.1 = (s32[16]{0:T(128)S(1)}, s32[16]{0:T(128)}, u32[]{:S(2)}) copy-start(s32[16]{0:T(128)} %param.7) | copy-start | bytes 196
  70.0 57.5 %copy-start = (f32[128,1024]{1,0:T(8,128)S(1)}, f32[128,1024]{1,0:T(8,128)}, u32[]{:S(2)}) copy-start(f32[128,1024]{1,0:T(8,128)} %get-tuple-element.7) | copy-start | bytes 1572868
  71.5 16.1 %all-to-all-start.3 = ((bf16[32,1,32]{2,1,0:T(2,128)(2,1)}), bf16[32,1,32]{2,1,0:T(2,128)(2,1)S(1)}, u32[]{:S(2)}, u32[]{:S(2)}) async-start(bf16[32,1,32]{2,1,0:T(2,128)(2,1)} %convert_element_type.45), calls=%async_computation.3 | async-start | bytes 32768 | tf_op jit(solution)/shard_map/all_to_all | solution.py:33
  87.5 12.4 %all-to-all-start.1 = ((bf16[32,2,1280]{2,1,0:T(2,128)(2,1)}), bf16[32,2,1280]{2,1,0:T(2,128)(2,1)S(1)}, u32[]{:S(2)}, u32[]{:S(2)}) async-start(bf16[32,2,1280]{2,1,0:T(2,128)(2,1)} %reshape.109), calls=%async_computation.1 | async-start | bytes 327680 | tf_op jit(solution)/shard_map/all_to_all | solution.py:33
  100.5 10.8 %all-to-all-start.4 = ((bf16[32,1,32]{2,1,0:T(2,128)(2,1)}), bf16[32,1,32]{2,1,0:T(2,128)(2,1)S(1)}, u32[]{:S(2)}, u32[]{:S(2)}) async-start(bf16[32,1,32]{2,1,0:T(2,128)(2,1)} %broadcast_in_dim.9), calls=%async_computation.4 | async-start | bytes 32768 | tf_op jit(solution)/shard_map/all_to_all | solution.py:50
  111.3 12.2 %all-to-all-start.2 = ((bf16[32,2,1280]{2,1,0:T(2,128)(2,1)}), bf16[32,2,1280]{2,1,0:T(2,128)(2,1)S(1)}, u32[]{:S(2)}, u32[]{:S(2)}) async-start(bf16[32,2,1280]{2,1,0:T(2,128)(2,1)} %reshape.111), calls=%async_computation.2 | async-start | bytes 327680 | tf_op jit(solution)/shard_map/all_to_all | solution.py:50
  123.5 21.1 %all-to-all-start = ((bf16[32,16,1024]{2,1,0:T(8,128)(2,1)}), bf16[32,16,1024]{2,1,0:T(8,128)(2,1)S(1)}, u32[]{:S(2)}, u32[]{:S(2)}) async-start(bf16[32,16,1024]{2,1,0:T(8,128)(2,1)} %bitcast.1), calls=%async_computation | async-start | bytes 2097152 | tf_op jit(solution)/shard_map/all_to_all | solution.py:33

commit v2 on v1

v2 whole, which is shorter than its diff:
```python
import jax
import jax.numpy as jnp
from jax import lax
from jax.experimental import pallas as pl
from jax.experimental.pallas import tpu as pltpu
from jax.sharding import Mesh
from jax.sharding import PartitionSpec as P

CLIENT = ("client_0", "client_1", "client_2")
EPSILON = 1e-06
MESH = pl.DeviceIdType.MESH

ORDER = ((2, 2), (2, 1), (2, 3), (2, 0), (1, 2), (3, 2), (0, 2), (1, 1), (3, 1), (0, 1), (1, 3), (3, 3), (0, 3), (1, 0), (3, 0), (0, 0))
STEPS = 16
BLOCK = 256
LANES = 128
YORDER = (2, 1, 3, 0)


def digits(values):
    return sum(v * 4**i for i, v in enumerate(values))


def kernel(
    pre_hbm, delta_hbm, weight_hbm, ids_ref, head_out, bias_out, embed_out, span_out,
    stage, low, low_t, weight, pre_b, hid_a, hid_b, slope, prod, crecv, acc_a, acc_b, sums, sums_low, yrecv, r_a, r_b, r_a2, r_b2,
    ids, emb, rest_own, rest_in, rest_all, picked, picked_in, squares, squares_zx, squares_y,
    delta_sem, weight_sem, pre_sem, c_send, c_recv, a_send, a_recv, b_send, b_recv, a2_send, a2_recv, b2_send, b2_recv, y_send, y_recv,
    i_send, i_recv, e_send, e_recv, rs_send, rs_recv, ag_send, ag_recv, p_send, p_recv, zx_send, zx_recv, sy_send, sy_recv,
):
    rows = low.shape[0]
    here = low.shape[1]
    clients = 16
    spans = rows // clients
    half = prod.shape[2] // 2
    z, x, c, y = (lax.axis_index(a) for a in (*CLIENT, "head"))

    def ring(one, offset):
        along_z = one * (1 - c) + (1 - one) * c
        return lax.rem(z + offset * along_z, 4), lax.rem(x + offset * (1 - along_z), 4), c, y

    def client_peer(o):
        return lax.rem(z + lax.div(o, 8), 4), lax.rem(x + lax.rem(lax.div(o, 2), 4), 4), lax.rem(c + lax.rem(o, 2), 2), y

    def plane_peer(o):
        return lax.rem(z + lax.div(o, 4), 4), lax.rem(x + lax.rem(o, 4), 4), c, y

    def column_peer(o):
        return z, x, lax.rem(c + lax.rem(o, 2), 2), lax.rem(y + lax.div(o, 2), 4)

    partner = (z, x, 1 - c, y)
    barrier = pltpu.get_barrier_semaphore()

    def greet(peer, first, last):
        def one(o, carry):
            pl.semaphore_signal(barrier, inc=1, device_id=peer(o), device_id_type=MESH)
            return carry

        lax.fori_loop(first, last, one, 0)

    greet(client_peer, 1, 32)
    greet(column_peer, 2, 8)

    def delta_copy(block):
        slot = block % 3
        return pltpu.make_async_copy(delta_hbm.at[pl.ds(block * 256, 256), :], stage.at[slot], delta_sem.at[slot])

    def chips(dp, dq):
        first = lax.rem(z + dp, 4) * 4 + lax.rem(x + dq, 4)
        second = lax.rem(z + dq, 4) * 4 + lax.rem(x + dp, 4)
        return first, second

    def pre_copies(dp, dq, slot):
        out = []
        for h, chip in enumerate(chips(dp, dq)):
            column = pl.multiple_of((chip * 2 + h) * LANES, LANES)
            out.append(
                pltpu.make_async_copy(
                    pre_hbm.at[:, pl.ds(column, LANES)],
                    pre_b.at[slot, :, pl.ds(h * LANES, LANES)],
                    pre_sem.at[slot, h],
                )
            )
        return out

    def weight_copy(part):
        size = weight.shape[0] // 4
        return pltpu.make_async_copy(weight_hbm.at[pl.ds(part * size, size), :], weight.at[pl.ds(part * size, size), :], weight_sem.at[part])

    def silu_to(slot, hid, at):
        for b in range(rows // 32):
            lines = pl.ds(b * 32, 32)
            v = pre_b[slot, lines, :].astype(jnp.float32)
            gate = 1.0 / (1.0 + jnp.exp(-v))
            value = v * gate
            hid[lines, :] = value.astype(jnp.bfloat16)
            slant = (gate + value * (1.0 - gate)).astype(jnp.bfloat16)
            for h in range(2):
                slope[at[h], lines, pl.ds(h * LANES, LANES)] = slant[:, h * LANES : (h + 1) * LANES]

    def remote(src, dst, send, recv, to):
        return pltpu.make_async_remote_copy(src_ref=src, dst_ref=dst, send_sem=send, recv_sem=recv, device_id=to, device_id_type=MESH)

    lower, upper = pl.ds(0, half), pl.ds(half, half)

    def core_copy(s):
        return remote(prod.at[s, 1 - c], crecv.at[s], c_send.at[s], c_recv.at[s], partner)

    def a_copies(i):
        return (
            remote(prod.at[i, c, lower], r_a.at[i, 0], a_send.at[i, 0], a_recv.at[i, 0], ring(1, 3)),
            remote(prod.at[i, c, upper], r_a.at[i, 1], a_send.at[i, 1], a_recv.at[i, 1], ring(1, 1)),
        )

    def b_copies(i):
        ahead, behind = 4 + 3 * i, 5 + 3 * i

        def one(chunk, part, side, k, to):
            return remote(prod.at[chunk, c, part], r_b.at[i, side, part], b_send.at[i, k], b_recv.at[i, k], to)

        return (
            one(ahead, lower, 0, 0, ring(1, 1)),
            one(behind, upper, 1, 1, ring(1, 3)),
            one(ahead, upper, 0, 2, ring(1, 1)),
            one(behind, lower, 1, 3, ring(1, 3)),
        )

    def a2_copies():
        chunk = 6
        return (
            remote(prod.at[chunk, c, lower], r_a2.at[0], a2_send.at[0], a2_recv.at[0], ring(0, 3)),
            remote(prod.at[chunk, c, upper], r_a2.at[1], a2_send.at[1], a2_recv.at[1], ring(0, 1)),
        )

    def b2_copies():
        def one(chunk, part, side, k, to):
            return remote(prod.at[chunk, c, part], r_b2.at[side, part], b2_send.at[k], b2_recv.at[k], to)

        return (
            one(9, lower, 0, 0, ring(0, 1)),
            one(12, upper, 1, 1, ring(0, 3)),
            one(9, upper, 0, 2, ring(0, 1)),
            one(12, lower, 1, 3, ring(0, 3)),
        )

    def y_copy(group):
        to = lax.rem(y + YORDER[group], 4)
        return remote(sums_low.at[pl.ds(4 * group, 4)], yrecv.at[group], y_send.at[group], y_recv.at[group], (z, x, c, to))

    def id_copies(stage_):
        if stage_ == 0:
            return [remote(ids.at[0, 0], ids.at[0, o], i_send.at[0, o], i_recv.at[0, o], ring(1, o)) for o in (2, 1, 3)]
        return [remote(ids.at[0], ids.at[o], i_send.at[1, o], i_recv.at[1, o], ring(0, o)) for o in (2, 1, 3)]

    def embed_copies(stage_):
        if stage_ == 0:
            return [remote(emb.at[0, 0], emb.at[0, o], e_send.at[0, o], e_recv.at[0, o], ring(1, o)) for o in (2, 1, 3)]
        return [remote(emb.at[0], emb.at[o], e_send.at[1, o], e_recv.at[1, o], ring(0, o)) for o in (2, 1, 3)]

    def piece_of(zz, xx, cc):
        return pl.ds(pl.multiple_of(zz * 32, 32), 32), pl.ds(pl.multiple_of((xx * 2 + cc) * LANES, LANES), LANES)

    def scatter_copy(o):
        to = client_peer(o)
        return remote(rest_own.at[piece_of(*to[:3])], rest_in.at[o], rs_send.at[o], rs_recv.at[o], to)

    def gather_copy(o):
        mine = piece_of(z, x, c)
        return remote(rest_all.at[mine], rest_all.at[mine], ag_send.at[o], ag_recv.at[o], client_peer(o))

    def picked_copy():
        return remote(picked, picked_in, p_send.at[0], p_recv.at[0], partner)

    def plane_copy(o):
        return remote(squares.at[0], squares_zx.at[o], zx_send.at[o], zx_recv.at[o], plane_peer(o))

    def column_copy(o):
        return remote(squares.at[1], squares_y.at[o], sy_send.at[o], sy_recv.at[o], column_peer(o))

    def over(first, last, what):
        def one(o, carry):
            what(o)
            return carry

        lax.fori_loop(first, last, one, 0)

    def start_all(copies):
        for copy in copies:
            copy.start()

    def arrive_all(copies):
        for copy in copies:
            copy.wait_recv()

    def core_add(s):
        core_copy(s).wait_recv()
        prod[s, c] = prod[s, c] + crecv[s]

    def do_b(i):
        first, second, third, fourth = b_copies(i)
        first.start()
        second.start()
        from_plus, from_minus = a_copies(i)
        ahead, behind = 4 + 3 * i, 5 + 3 * i
        from_minus.wait_recv()
        prod[ahead, c, upper] = prod[ahead, c, upper] + r_a[i, 1]
        from_plus.wait_recv()
        prod[behind, c, lower] = prod[behind, c, lower] + r_a[i, 0]
        third.start()
        fourth.start()

    def three(a, b, d):
        return a.astype(jnp.float32) + b.astype(jnp.float32) + d.astype(jnp.float32)

    def do_f(i):
        arrive_all(b_copies(i))
        chunk = 6 + 3 * i
        prod[chunk, c] = three(prod[chunk, c], r_b[i, 0], r_b[i, 1]).astype(jnp.bfloat16)

    def do_b2():
        first, second, third, fourth = b2_copies()
        first.start()
        second.start()
        from_plus, from_minus = a2_copies()
        from_minus.wait_recv()
        prod[9, c, upper] = prod[9, c, upper] + r_a2[1]
        from_plus.wait_recv()
        prod[12, c, lower] = prod[12, c, lower] + r_a2[0]
        third.start()
        fourth.start()

    def do_final():
        arrive_all(b2_copies())
        whole = three(prod[15, c], r_b2[0], r_b2[1])
        squares[0, pl.ds(0, 1), :] = jnp.sum(whole * whole, axis=0, keepdims=True)
        head_out[...] = whole.T

    start_all(pre_copies(*ORDER[0], 0))
    for block in range(3):
        delta_copy(block).start()
    for s in range(1, 4):
        start_all(pre_copies(*ORDER[s], s))
    for client in range(clients):
        ids[0, 0, pl.ds(client, 1), :] = jnp.full((1, LANES), ids_ref[client], jnp.int32)
    squares[...] = jnp.zeros(squares.shape, jnp.float32)
    rest_own[pl.ds(96, 32), :] = jnp.zeros((32, here), jnp.bfloat16)
    for copy in pre_copies(*ORDER[0], 0):
        copy.wait()
    silu_to(0, hid_a, chips(*ORDER[0]))
    start_all(pre_copies(*ORDER[4], 0))
    bias = jnp.zeros((1, here), jnp.float32)
    for block in range(rows // 256):
        delta_copy(block).wait()
        lines = pl.ds(block * 256, 256)
        values = stage[block % 3]
        bias = bias + jnp.sum(values, axis=0, keepdims=True)
        rounded = values.astype(jnp.bfloat16)
        low[lines, :] = rounded
        low_t[:, lines] = rounded.T
        if block + 3 < rows // 256:
            delta_copy(block + 3).start()
    first_line = lax.broadcasted_iota(jnp.int32, (16, here), 0) == 0
    rest_own[pl.ds(80, 16), :] = jnp.where(first_line, jnp.broadcast_to(bias, (16, here)), 0.0).astype(jnp.bfloat16)
    for part in range(4):
        weight_copy(part).start()
    pl.semaphore_wait(barrier, 37)
    start_all(id_copies(0))

    next_p, next_q = digits([o[0] for o in ORDER[1:]]), digits([o[1] for o in ORDER[1:]])
    load_p, load_q = digits([o[0] for o in ORDER[5:]]), digits([o[1] for o in ORDER[5:]])

    def first_product(i, carry):
        np_, nq_, lp_, lq_ = carry
        offsets, slots = [], []
        for k in range(2):
            offsets.append((lax.rem(np_, 4), lax.rem(nq_, 4)))
            slots.append(lax.rem(2 * i + k + 1, 4))
            np_, nq_ = lax.div(np_, 4), lax.div(nq_, 4)

        def arrived(k):
            for copy in pre_copies(*offsets[k], slots[k]):
                copy.wait()

        arrived(0)
        pl.when(i < STEPS // 2 - 1)(lambda: arrived(1))
        last = lax.div(i, STEPS // 2 - 1)
        for k, (now, later) in enumerate(((hid_a, hid_b), (hid_b, hid_a))):
            s = 2 * i + k
            spare = last if k == 1 else 0
            at = [chip * (1 - spare) + STEPS * spare for chip in chips(*offsets[k])]
            silu_to(slots[k], later, at)
            product = jnp.dot(low_t[...], now[...], preferred_element_type=jnp.float32).astype(jnp.bfloat16)
            for h in range(2):
                prod[s, h] = product[:, h * LANES : (h + 1) * LANES]

        core_copy(2 * i).start()
        core_copy(2 * i + 1).start()
        for k in range(2):

            @pl.when(2 * i + k + 5 < STEPS)
            def _(k=k, lp_=lp_, lq_=lq_):
                start_all(pre_copies(lax.rem(lp_, 4), lax.rem(lq_, 4), slots[k]))

            lp_, lq_ = lax.div(lp_, 4), lax.div(lq_, 4)

        @pl.when(i == 0)
        def _():
            arrive_all(id_copies(0))
            start_all(id_copies(1))

        @pl.when(i >= 1)
        def _():
            core_add(2 * i - 2)
            core_add(2 * i - 1)

        @pl.when(i == 1)
        def _():
            start_all(a_copies(0))
            start_all(a_copies(1))

        @pl.when(i == 2)
        def _():
            start_all(a_copies(2))
            start_all(a_copies(3))

        pl.when(i == 3)(lambda: do_b(0))
        pl.when(i == 5)(lambda: do_b(1))

        @pl.when(i == 6)
        def _():
            do_b(2)
            do_f(0)
            start_all(a2_copies())

        return np_, nq_, lp_, lq_

    lax.fori_loop(0, STEPS // 2, first_product, tuple(jnp.int32(t) for t in (next_p, next_q, load_p, load_q)))

    def reduce_rows(acc, chunk, u):
        span = jnp.zeros((spans, BLOCK), jnp.float32)
        for client in range(clients):
            lines = pl.ds(client * spans, spans)
            grad = acc[lines, :] * slope[chunk, lines, :].astype(jnp.float32)
            span = span + grad
            sums[u, pl.ds(spans + client, 1), :] = jnp.sum(grad, axis=0, keepdims=True)
        sums[u, pl.ds(0, spans), :] = span

    for part in range(4):
        weight_copy(part).wait()

    def second_product(g, carry):
        before, table = carry
        chunk0 = lax.rem(y + lax.rem(table, 4), 4) * 4
        for t in range(4):
            u = 4 * g + t
            now, last = (acc_a, acc_b) if t % 2 == 0 else (acc_b, acc_a)
            chunk = chunk0 + t
            previous = before if t == 0 else chunk - 1
            slot = lax.rem(u + STEPS, STEPS + 1)
            reduce_rows(last, previous, slot)
            lines = pl.ds(pl.multiple_of(chunk * BLOCK, BLOCK), BLOCK)
            now[...] = lax.dot_general(low[...], weight[lines, :], (((1,), (1,)), ((), ())), preferred_element_type=jnp.float32)
            if t == 1:

                @pl.when(g == 0)
                def _():
                    core_add(STEPS - 2)
                    core_add(STEPS - 1)
                    do_b(3)
                    do_f(1)

                for group in range(3):

                    @pl.when(g == group + 1)
                    def _(group=group):
                        for k in range(4):
                            sums_low[4 * group + k] = sums[4 * group + k].astype(jnp.bfloat16)
                        y_copy(group).start()

                @pl.when(g == 1)
                def _():
                    do_f(2)
                    do_b2()

                pl.when(g == 2)(lambda: do_f(3))
            elif t == 3:
                pl.when(g == 2)(do_final)
        return chunk0 + 3, lax.div(table, 4)

    final_chunk, _ = lax.fori_loop(0, 4, second_product, (jnp.int32(0), jnp.int32(digits(YORDER))))
    reduce_rows(acc_b, final_chunk, STEPS - 1)

    for group in range(3):
        y_copy(group).wait_recv()
    embed_square = jnp.zeros((1, LANES), jnp.float32)
    for t in range(4):
        total = sums[12 + t]
        for group in range(3):
            total = total + yrecv[group, t].astype(jnp.float32)
        lanes = pl.ds(t * BLOCK, BLOCK)
        rest_own[pl.ds(0, spans), lanes] = total[:spans].astype(jnp.bfloat16)
        mine = total[spans:]
        emb[0, 0, :, lanes] = mine.astype(jnp.bfloat16)
        square = jnp.sum(mine * mine, axis=0, keepdims=True)
        embed_square = embed_square + square[:, :LANES] + square[:, LANES:]
    squares[0, pl.ds(1, 1), :] = embed_square
    over(1, 32, lambda o: scatter_copy(o).start())
    start_all(embed_copies(0))
    over(1, 32, lambda o: scatter_copy(o).wait_recv())
    piece = rest_own[piece_of(z, x, c)].astype(jnp.float32)
    piece = piece + jnp.sum(rest_in[1:].astype(jnp.float32), axis=0)
    rest_all[piece_of(z, x, c)] = piece.astype(jnp.bfloat16)
    squares[0, pl.ds(2, 1), :] = jnp.sum(piece * piece, axis=0, keepdims=True)
    over(1, 32, lambda o: gather_copy(o).start())
    over(1, 16, lambda o: plane_copy(o).start())
    arrive_all(embed_copies(0))
    start_all(embed_copies(1))
    over(1, 16, lambda o: plane_copy(o).wait_recv())
    squares[1] = squares[0] + jnp.sum(squares_zx[1:], axis=0)
    over(1, 8, lambda o: column_copy(o).start())
    over(1, 32, lambda o: gather_copy(o).wait_recv())
    arrive_all(id_copies(1))
    lane = lax.broadcasted_iota(jnp.int32, (1, LANES), 1)
    chip = (z * 4 + x) * 2
    wanted = jnp.where(lane < clients, (chip + c) * clients + lane, jnp.where(lane < 2 * clients, (chip + 1 - c) * clients + lane - clients, -1))
    chosen = (ids[...].reshape(16 * clients, LANES) == wanted).astype(jnp.float32).astype(jnp.bfloat16)
    arrive_all(embed_copies(1))
    table = lax.dot_general(chosen, emb[...].reshape(16 * clients, here), (((0,), (0,)), ((), ())), preferred_element_type=jnp.float32)
    picked[...] = table[clients : 2 * clients].astype(jnp.bfloat16)
    picked_copy().start()
    over(1, 8, lambda o: column_copy(o).wait_recv())
    totals = squares[1] + jnp.sum(squares_y[1:], axis=0)

    def factor(line, number):
        total = jnp.sum(totals[line : line + 1], axis=1, keepdims=True)
        return jnp.minimum(1.0, 1.0 / jnp.sqrt(total / number + EPSILON))

    width = weight.shape[0]
    emit = here * 4
    head_out[...] = head_out[...] * factor(0, width * emit)
    rest = factor(2, spans * width + emit)
    span_out[...] = rest_all[pl.ds(0, spans), :].astype(jnp.float32) * rest
    bias_out[...] = rest_all[pl.ds(spans, 16), :].astype(jnp.float32)[:1] * rest
    embed_factor = factor(1, 32 * clients * width)
    picked_copy().wait_recv()
    embed_out[...] = (table[:clients] + picked_in[...].astype(jnp.float32)) * embed_factor

    over(0, STEPS, lambda s: core_copy(s).wait_send())
    sent = [*a2_copies(), *b2_copies(), picked_copy()]
    for i in range(4):
        sent += [*a_copies(i), *b_copies(i)]
    for group in range(3):
        sent.append(y_copy(group))
    for k in range(2):
        sent += [*id_copies(k), *embed_copies(k)]
    for copy in sent:
        copy.wait_send()
    over(1, 32, lambda o: scatter_copy(o).wait_send())
    over(1, 32, lambda o: gather_copy(o).wait_send())
    over(1, 16, lambda o: plane_copy(o).wait_send())
    over(1, 8, lambda o: column_copy(o).wait_send())


def per_device(pre, delta, head_weight, client_ids):
    rows, width = pre.shape
    here = delta.shape[1]
    clients = client_ids.shape[0]
    bf16, f32 = jnp.bfloat16, jnp.float32
    dma = pltpu.SemaphoreType.DMA
    spans = rows // clients
    anywhere = pl.BlockSpec(memory_space=pl.ANY)
    in_vmem = pl.BlockSpec(memory_space=pltpu.VMEM)
    head, bias, embed, span = pl.pallas_call(
        kernel,
        name="products",
        out_shape=(
            jax.ShapeDtypeStruct((LANES, here), f32),
            jax.ShapeDtypeStruct((1, here), f32),
            jax.ShapeDtypeStruct((clients, here), f32),
            jax.ShapeDtypeStruct((spans, here), f32),
        ),
        in_specs=[anywhere] * 3 + [pl.BlockSpec(memory_space=pltpu.SMEM)],
        out_specs=[in_vmem] * 4,
        scratch_shapes=[
            pltpu.VMEM((3, 256, here), f32),
            pltpu.VMEM((rows, here), bf16),
            pltpu.VMEM((here, rows), bf16),
            pltpu.VMEM((width, here), bf16),
            pltpu.VMEM((4, rows, BLOCK), bf16),
            pltpu.VMEM((rows, BLOCK), bf16),
            pltpu.VMEM((rows, BLOCK), bf16),
            pltpu.VMEM((STEPS + 1, rows, BLOCK), bf16),
            pltpu.VMEM((STEPS, 2, here, LANES), bf16),
            pltpu.VMEM((STEPS, here, LANES), bf16),
            pltpu.VMEM((rows, BLOCK), f32),
            pltpu.VMEM((rows, BLOCK), f32),
            pltpu.VMEM((STEPS + 1, spans + 16, BLOCK), f32),
            pltpu.VMEM((12, spans + 16, BLOCK), bf16),
            pltpu.VMEM((3, 4, spans + 16, BLOCK), bf16),
            pltpu.VMEM((4, 2, here // 2, LANES), bf16),
            pltpu.VMEM((4, 2, here, LANES), bf16),
            pltpu.VMEM((2, here // 2, LANES), bf16),
            pltpu.VMEM((2, here, LANES), bf16),
            pltpu.VMEM((4, 4, clients, LANES), jnp.int32),
            pltpu.VMEM((4, 4, clients, here), bf16),
            pltpu.VMEM((128, here), bf16),
            pltpu.VMEM((32, 32, LANES), bf16),
            pltpu.VMEM((128, here), bf16),
            pltpu.VMEM((clients, here), bf16),
            pltpu.VMEM((clients, here), bf16),
            pltpu.VMEM((2, 8, LANES), f32),
            pltpu.VMEM((16, 8, LANES), f32),
            pltpu.VMEM((8, 8, LANES), f32),
            dma((3,)),
            dma((4,)),
            dma((4, 2)),
            *[dma((STEPS,))] * 2,
            *[dma((4, 2))] * 2,
            *[dma((4, 4))] * 2,
            *[dma((2,))] * 2,
            *[dma((4,))] * 2,
            *[dma((3,))] * 2,
            *[dma((2, 4))] * 4,
            *[dma((32,))] * 4,
            *[dma((1,))] * 2,
            *[dma((16,))] * 2,
            *[dma((8,))] * 2,
        ],
        compiler_params=pltpu.CompilerParams(collective_id=0, has_side_effects=True, vmem_limit_bytes=67_000_000),
    )(pre, delta, head_weight, client_ids)
    return head, bias[0], embed, span


def solution(mesh):
    torus = Mesh(
        mesh.devices.reshape(4, 4, 2, mesh.shape["head"]),
        ("client_0", "client_1", "client_2", "head"),
    )
    return jax.shard_map(
        per_device,
        mesh=torus,
        in_specs=(P(CLIENT, None), P(CLIENT, "head"), P(None, "head"), P(CLIENT)),
        out_specs=(P(CLIENT, "head"), P("head"), P(CLIENT, "head"), P(None, "head")),
        check_vma=False,
    )
```

time: 173 us -> 80.4 us (0.46)
  waiting for transfers between devices: 33.2 us -> 0 us
  starting transfers between devices: 25.5 us -> 0 us
  blocking collectives: 18.2 us -> 0 us
  other arithmetic: 11.5 us -> 0 us
  Pallas kernels: 69.3 us -> 73.1 us
  between operations: 4.18 us -> 0.64 us
  matrix products: 2.79 us -> 0 us
    all_to_all x5 -> x0, waiting for transfers between devices: 33.2 us -> none  [the longest x3 23.9 us: sum_at_owner(): lax.all_to_all(tiles, axis, split_axis=0, concat_axis=0, tiled=True)]
    all_to_all x5 -> x0, starting transfers between devices: 25.5 us -> none  [the longest x3 17.5 us: sum_at_owner(): lax.all_to_all(tiles, axis, split_axis=0, concat_axis=0, tiled=True)]
    all_to_all x2 -> x0, blocking collectives: 18.2 us -> none  [sent_to_all(): lax.all_to_all(jnp.broadcast_to(x[None], (peers, *x.shape)), axis, 0, 0,...]
    unnamed x8 -> x4, local copies, waits for them, and re-layouts: 1.67 us -> 6.35 us
    reduce_sum x9 -> x0, other arithmetic: 3.79 us -> none  [the longest x1 1.27 us: per_device(): jnp.sum(span_raw * span_raw) + jnp.sum(bias_raw * bias_raw)]
    pallas_call x1, Pallas kernels: 69.3 us -> 73.1 us  [per_device(): pl.pallas_call(kernel, name='products', out_shape=(jax.ShapeDtypeStruct((...]
    dot_general x1 -> x0, matrix products: 2.79 us -> none  [per_device(): jnp.dot(selector, client_part, precision=lax.Precision.HIGHEST, preferred...]
    mul x4 -> x0, other arithmetic: 2.39 us -> none  [the longest x1 0.9 us: per_device(): rest_factor * span_raw]
  transfers between devices with their start and end apart: 5 -> 0, of which waited for: 5 -> 0; matrix products, arithmetic and copies ran while one was open for 7% -> 0% of each run, Pallas kernels for 0% -> 0%
where the time goes in v2:
time: 80.4 us; the launch traced here: 80.1 us
  Pallas kernels  73.1 us (91%)
  local copies, waits for them, and re-layouts  6.35 us (8%)
    pallas_call x1, Pallas kernels, per_device(): pl.pallas_call(kernel, name='products', out_shape=(jax.ShapeDtypeStruct((...  73.1 us
    unnamed x4, local copies, waits for them, and re-layouts  6.35 us

profile of v2, /device:TPU:1, one launch (start us, length us, event | category | flops | bytes accessed | tf_op | source)
XLA Modules:
  0.0 80.1 jit_solution(12608073407679572685)
XLA Ops:
  0.6 73.1 %products.1 = (f32[128,1024]{1,0:T(8,128)}, f32[1,1024]{1,0:T(1,128)}, f32[16,1024]{1,0:T(8,128)}, f32[80,1024]{1,0:T(8,128)}) custom-call(bf16[1280,4096]{1,0:T(8,128)(2,1)} %pre_hbm.1, f32[1280,1024]{1,0:T(8,128)} %delta_hbm.1, bf16[4096,1024]{1,0:T(8,128)(2,1)} %weight_hbm.1, s32[16]{0:T(128)} %ids_ref.1), custom_call_target="tpu_custom_call" | custom-call | tf_op jit(solution)/shard_map/products/pallas_call | solution.py:473
  73.8 1.9 %copy.12 = f32[128,1024]{1,0:T(8,128)} copy(f32[128,1024]{1,0:T(8,128)} %get-tuple-element.16) | data formatting | bytes 1048576
  75.7 1.3 %copy.13 = f32[1024]{0:T(1024)} copy(f32[1024]{0:T(1024)} %bitcast.1) | data formatting | bytes 8192
  76.9 1.5 %copy.14 = f32[16,1024]{1,0:T(8,128)} copy(f32[16,1024]{1,0:T(8,128)} %get-tuple-element.18) | data formatting | bytes 131072
  78.4 1.7 %copy.15 = f32[80,1024]{1,0:T(8,128)} copy(f32[80,1024]{1,0:T(8,128)} %get-tuple-element.19) | data formatting | bytes 655360

commit v3 on v2

--- a/solution.py
+++ b/solution.py
@@ -22,10 +22,10 @@
 
 
 def kernel(
-    pre_hbm, delta_hbm, weight_hbm, ids_ref, head_out, bias_out, embed_out, span_out,
-    stage, low, low_t, weight, pre_b, hid_a, hid_b, slope, prod, crecv, acc_a, acc_b, sums, sums_low, yrecv, r_a, r_b, r_a2, r_b2,
+    pre_hbm, delta_hbm, weight_hbm, ids_ref, head_out, rest_out, embed_out, total_out,
+    stage, low, low_t, weight, pre_b, hid_a, hid_b, slope, prod, crecv, acc_a, acc_b, sums, span_low, rows_low, span_in, rows_in, own_send, own_in, bias_rows, r_a, r_b, r_a2, r_b2,
     ids, emb, rest_own, rest_in, rest_all, picked, picked_in, squares, squares_zx, squares_y,
-    delta_sem, weight_sem, pre_sem, c_send, c_recv, a_send, a_recv, b_send, b_recv, a2_send, a2_recv, b2_send, b2_recv, y_send, y_recv,
+    delta_sem, weight_sem, pre_sem, c_send, c_recv, a_send, a_recv, b_send, b_recv, a2_send, a2_recv, b2_send, b2_recv, y_send, y_recv, ys_send, ys_recv, own_sems,
     i_send, i_recv, e_send, e_recv, rs_send, rs_recv, ag_send, ag_recv, p_send, p_recv, zx_send, zx_recv, sy_send, sy_recv,
 ):
     rows = low.shape[0]
@@ -143,9 +143,28 @@
             one(12, lower, 1, 3, ring(0, 3)),
         )
 
-    def y_copy(group):
-        to = lax.rem(y + YORDER[group], 4)
-        return remote(sums_low.at[pl.ds(4 * group, 4)], yrecv.at[group], y_send.at[group], y_recv.at[group], (z, x, c, to))
+    def y_target(group):
+        return lax.rem(y + YORDER[group], 4)
+
+    def y_rows(group):
+        return remote(rows_low.at[group], rows_in.at[group], y_send.at[group], y_recv.at[group], (z, x, c, y_target(group)))
+
+    def y_spans(group, side):
+        mine = span_low.at[pl.ds(4 * group + 2 * side, 2)]
+        return remote(mine, span_in.at[group, c], ys_send.at[group, side], ys_recv.at[group, c], (z, x, side, y_target(group)))
+
+    def y_arrival(group, core):
+        mine = span_low.at[pl.ds(4 * group, 2)]
+        return remote(mine, span_in.at[group, core], ys_send.at[group, core], ys_recv.at[group, core], (z, x, core, y_target(group)))
+
+    def own_copy():
+        return remote(own_send, own_in, own_sems.at[0], own_sems.at[1], partner)
+
+    def send_spans(group, side):
+        for k in range(2):
+            chunk = 4 * group + 2 * side + k
+            span_low[chunk] = sums[chunk, pl.ds(0, spans), :].astype(jnp.bfloat16)
+        y_spans(group, side).start()
 
     def id_copies(stage_):
         if stage_ == 0:
@@ -157,15 +176,15 @@
             return [remote(emb.at[0, 0], emb.at[0, o], e_send.at[0, o], e_recv.at[0, o], ring(1, o)) for o in (2, 1, 3)]
         return [remote(emb.at[0], emb.at[o], e_send.at[1, o], e_recv.at[1, o], ring(0, o)) for o in (2, 1, 3)]
 
-    def piece_of(zz, xx, cc):
-        return pl.ds(pl.multiple_of(zz * 32, 32), 32), pl.ds(pl.multiple_of((xx * 2 + cc) * LANES, LANES), LANES)
+    def piece_of(line, tile):
+        return pl.ds(pl.multiple_of(line * 32, 32), 32), pl.ds(pl.multiple_of(tile * LANES, LANES), LANES)
 
     def scatter_copy(o):
-        to = client_peer(o)
-        return remote(rest_own.at[piece_of(*to[:3])], rest_in.at[o], rs_send.at[o], rs_recv.at[o], to)
+        to = plane_peer(o)
+        return remote(rest_own.at[piece_of(to[0], to[1])], rest_in.at[o], rs_send.at[o], rs_recv.at[o], to)
 
     def gather_copy(o):
-        mine = piece_of(z, x, c)
+        mine = piece_of(z, c * 4 + x)
         return remote(rest_all.at[mine], rest_all.at[mine], ag_send.at[o], ag_recv.at[o], client_peer(o))
 
     def picked_copy():
@@ -243,7 +262,7 @@
     for client in range(clients):
         ids[0, 0, pl.ds(client, 1), :] = jnp.full((1, LANES), ids_ref[client], jnp.int32)
     squares[...] = jnp.zeros(squares.shape, jnp.float32)
-    rest_own[pl.ds(96, 32), :] = jnp.zeros((32, here), jnp.bfloat16)
+    rest_own[pl.ds(96, 32), :] = jnp.zeros((32, here // 2), jnp.bfloat16)
     for copy in pre_copies(*ORDER[0], 0):
         copy.wait()
     silu_to(0, hid_a, chips(*ORDER[0]))
@@ -260,11 +279,9 @@
         if block + 3 < rows // 256:
             delta_copy(block + 3).start()
     first_line = lax.broadcasted_iota(jnp.int32, (16, here), 0) == 0
-    rest_own[pl.ds(80, 16), :] = jnp.where(first_line, jnp.broadcast_to(bias, (16, here)), 0.0).astype(jnp.bfloat16)
+    bias_rows[...] = jnp.where(first_line, jnp.broadcast_to(bias, (16, here)), 0.0)
     for part in range(4):
         weight_copy(part).start()
-    pl.semaphore_wait(barrier, 37)
-    start_all(id_copies(0))
 
     next_p, next_q = digits([o[0] for o in ORDER[1:]]), digits([o[1] for o in ORDER[1:]])
     load_p, load_q = digits([o[0] for o in ORDER[5:]]), digits([o[1] for o in ORDER[5:]])
@@ -293,6 +310,11 @@
             for h in range(2):
                 prod[s, h] = product[:, h * LANES : (h + 1) * LANES]
 
+        @pl.when(i == 0)
+        def _():
+            pl.semaphore_wait(barrier, 37)
+            start_all(id_copies(0))
+
         core_copy(2 * i).start()
         core_copy(2 * i + 1).start()
         for k in range(2):
@@ -303,7 +325,7 @@
 
             lp_, lq_ = lax.div(lp_, 4), lax.div(lq_, 4)
 
-        @pl.when(i == 0)
+        @pl.when(i == 1)
         def _():
             arrive_all(id_copies(0))
             start_all(id_copies(1))
@@ -373,9 +395,10 @@
 
                     @pl.when(g == group + 1)
                     def _(group=group):
+                        send_spans(group, 1)
                         for k in range(4):
-                            sums_low[4 * group + k] = sums[4 * group + k].astype(jnp.bfloat16)
-                        y_copy(group).start()
+                            rows_low[group, k] = sums[4 * group + k, pl.ds(spans, clients), :].astype(jnp.bfloat16)
+                        y_rows(group).start()
 
                 @pl.when(g == 1)
                 def _():
@@ -384,32 +407,49 @@
 
                 pl.when(g == 2)(lambda: do_f(3))
             elif t == 3:
+                for group in range(3):
+                    pl.when(g == group)(lambda group=group: send_spans(group, 0))
                 pl.when(g == 2)(do_final)
         return chunk0 + 3, lax.div(table, 4)
 
     final_chunk, _ = lax.fori_loop(0, 4, second_product, (jnp.int32(0), jnp.int32(digits(YORDER))))
     reduce_rows(acc_b, final_chunk, STEPS - 1)
 
+    half_here = here // 2
+    for t in range(2):
+        lanes = pl.ds(pl.multiple_of((1 - c) * half_here + t * BLOCK, BLOCK), BLOCK)
+        own_send[t, pl.ds(0, spans), :] = sums[12 + 2 * (1 - c) + t, pl.ds(0, spans), :].astype(jnp.bfloat16)
+        own_send[t, pl.ds(spans, 16), :] = bias_rows[:, lanes].astype(jnp.bfloat16)
+    own_copy().start()
     for group in range(3):
-        y_copy(group).wait_recv()
+        y_rows(group).wait_recv()
+        for core in range(2):
+            y_arrival(group, core).wait_recv()
     embed_square = jnp.zeros((1, LANES), jnp.float32)
     for t in range(4):
-        total = sums[12 + t]
+        mine = sums[12 + t, pl.ds(spans, clients), :]
         for group in range(3):
-            total = total + yrecv[group, t].astype(jnp.float32)
-        lanes = pl.ds(t * BLOCK, BLOCK)
-        rest_own[pl.ds(0, spans), lanes] = total[:spans].astype(jnp.bfloat16)
-        mine = total[spans:]
-        emb[0, 0, :, lanes] = mine.astype(jnp.bfloat16)
+            mine = mine + rows_in[group, t].astype(jnp.float32)
+        emb[0, 0, :, pl.ds(t * BLOCK, BLOCK)] = mine.astype(jnp.bfloat16)
         square = jnp.sum(mine * mine, axis=0, keepdims=True)
         embed_square = embed_square + square[:, :LANES] + square[:, LANES:]
+    own_copy().wait_recv()
+    for t in range(2):
+        total = sums[12 + 2 * c + t, pl.ds(0, spans), :] + own_in[t, pl.ds(0, spans), :].astype(jnp.float32)
+        for group in range(3):
+            for core in range(2):
+                total = total + span_in[group, core, t].astype(jnp.float32)
+        lanes = pl.ds(t * BLOCK, BLOCK)
+        rest_own[pl.ds(0, spans), lanes] = total.astype(jnp.bfloat16)
+        mine = bias_rows[:, pl.ds(pl.multiple_of(c * half_here + t * BLOCK, BLOCK), BLOCK)]
+        rest_own[pl.ds(spans, 16), lanes] = (mine + own_in[t, pl.ds(spans, 16), :].astype(jnp.float32)).astype(jnp.bfloat16)
     squares[0, pl.ds(1, 1), :] = embed_square
-    over(1, 32, lambda o: scatter_copy(o).start())
+    over(1, 16, lambda o: scatter_copy(o).start())
     start_all(embed_copies(0))
-    over(1, 32, lambda o: scatter_copy(o).wait_recv())
-    piece = rest_own[piece_of(z, x, c)].astype(jnp.float32)
+    over(1, 16, lambda o: scatter_copy(o).wait_recv())
+    piece = rest_own[piece_of(z, x)].astype(jnp.float32)
     piece = piece + jnp.sum(rest_in[1:].astype(jnp.float32), axis=0)
-    rest_all[piece_of(z, x, c)] = piece.astype(jnp.bfloat16)
+    rest_all[piece_of(z, c * 4 + x)] = piece.astype(jnp.bfloat16)
     squares[0, pl.ds(2, 1), :] = jnp.sum(piece * piece, axis=0, keepdims=True)
     over(1, 32, lambda o: gather_copy(o).start())
     over(1, 16, lambda o: plane_copy(o).start())
@@ -429,36 +469,40 @@
     picked[...] = table[clients : 2 * clients].astype(jnp.bfloat16)
     picked_copy().start()
     over(1, 8, lambda o: column_copy(o).wait_recv())
-    totals = squares[1] + jnp.sum(squares_y[1:], axis=0)
-
-    def factor(line, number):
-        total = jnp.sum(totals[line : line + 1], axis=1, keepdims=True)
-        return jnp.minimum(1.0, 1.0 / jnp.sqrt(total / number + EPSILON))
-
-    width = weight.shape[0]
-    emit = here * 4
-    head_out[...] = head_out[...] * factor(0, width * emit)
-    rest = factor(2, spans * width + emit)
-    span_out[...] = rest_all[pl.ds(0, spans), :].astype(jnp.float32) * rest
-    bias_out[...] = rest_all[pl.ds(spans, 16), :].astype(jnp.float32)[:1] * rest
-    embed_factor = factor(1, 32 * clients * width)
+    total_out[...] = squares[1] + jnp.sum(squares_y[1:], axis=0)
+    rest_out[...] = rest_all[pl.ds(0, spans + 16), :]
     picked_copy().wait_recv()
-    embed_out[...] = (table[:clients] + picked_in[...].astype(jnp.float32)) * embed_factor
+    embed_out[...] = table[:clients] + picked_in[...].astype(jnp.float32)
 
     over(0, STEPS, lambda s: core_copy(s).wait_send())
-    sent = [*a2_copies(), *b2_copies(), picked_copy()]
+    sent = [*a2_copies(), *b2_copies(), picked_copy(), own_copy()]
     for i in range(4):
         sent += [*a_copies(i), *b_copies(i)]
     for group in range(3):
-        sent.append(y_copy(group))
+        sent += [y_rows(group), y_spans(group, 0), y_spans(group, 1)]
     for k in range(2):
         sent += [*id_copies(k), *embed_copies(k)]
     for copy in sent:
         copy.wait_send()
-    over(1, 32, lambda o: scatter_copy(o).wait_send())
+    over(1, 16, lambda o: scatter_copy(o).wait_send())
     over(1, 32, lambda o: gather_copy(o).wait_send())
     over(1, 16, lambda o: plane_copy(o).wait_send())
     over(1, 8, lambda o: column_copy(o).wait_send())
+
+
+def scale(head, rest, embed, total, head_out, bias_out, embed_out, span_out):
+    spans, here = span_out.shape
+    width, emit = here * 4, here * 4
+
+    def factor(line, number):
+        whole = jnp.sum(total[pl.ds(line, 1), :], axis=1, keepdims=True)
+        return jnp.minimum(1.0, 1.0 / jnp.sqrt(whole / number + EPSILON))
+
+    head_out[...] = head[...] * factor(0, width * emit)
+    embed_out[...] = embed[...] * factor(1, 32 * embed.shape[0] * width)
+    small = factor(2, spans * width + emit)
+    span_out[...] = rest[pl.ds(0, spans), :].astype(jnp.float32) * small
+    bias_out[...] = rest[pl.ds(spans, 16), :].astype(jnp.float32)[:1] * small
 
 
 def per_device(pre, delta, head_weight, client_ids):
@@ -470,14 +514,14 @@
     spans = rows // clients
     anywhere = pl.BlockSpec(memory_space=pl.ANY)
     in_vmem = pl.BlockSpec(memory_space=pltpu.VMEM)
-    head, bias, embed, span = pl.pallas_call(
+    head, rest, embed, total = pl.pallas_call(
         kernel,
         name="products",
         out_shape=(
             jax.ShapeDtypeStruct((LANES, here), f32),
-            jax.ShapeDtypeStruct((1, here), f32),
+            jax.ShapeDtypeStruct((spans + 16, here), bf16),
             jax.ShapeDtypeStruct((clients, here), f32),
-            jax.ShapeDtypeStruct((spans, here), f32),
+            jax.ShapeDtypeStruct((8, LANES), f32),
         ),
         in_specs=[anywhere] * 3 + [pl.BlockSpec(memory_space=pltpu.SMEM)],
         out_specs=[in_vmem] * 4,
@@ -495,16 +539,21 @@
             pltpu.VMEM((rows, BLOCK), f32),
             pltpu.VMEM((rows, BLOCK), f32),
             pltpu.VMEM((STEPS + 1, spans + 16, BLOCK), f32),
-            pltpu.VMEM((12, spans + 16, BLOCK), bf16),
-            pltpu.VMEM((3, 4, spans + 16, BLOCK), bf16),
+            pltpu.VMEM((12, spans, BLOCK), bf16),
+            pltpu.VMEM((3, 4, clients, BLOCK), bf16),
+            pltpu.VMEM((3, 2, 2, spans, BLOCK), bf16),
+            pltpu.VMEM((3, 4, clients, BLOCK), bf16),
+            pltpu.VMEM((2, spans + 16, BLOCK), bf16),
+            pltpu.VMEM((2, spans + 16, BLOCK), bf16),
+            pltpu.VMEM((16, here), f32),
             pltpu.VMEM((4, 2, here // 2, LANES), bf16),
             pltpu.VMEM((4, 2, here, LANES), bf16),
             pltpu.VMEM((2, here // 2, LANES), bf16),
             pltpu.VMEM((2, here, LANES), bf16),
             pltpu.VMEM((4, 4, clients, LANES), jnp.int32),
             pltpu.VMEM((4, 4, clients, here), bf16),
-            pltpu.VMEM((128, here), bf16),
-            pltpu.VMEM((32, 32, LANES), bf16),
+            pltpu.VMEM((128, here // 2), bf16),
+            pltpu.VMEM((16, 32, LANES), bf16),
             pltpu.VMEM((128, here), bf16),
             pltpu.VMEM((clients, here), bf16),
             pltpu.VMEM((clients, here), bf16),
@@ -520,14 +569,29 @@
             *[dma((2,))] * 2,
             *[dma((4,))] * 2,
             *[dma((3,))] * 2,
+            *[dma((3, 2))] * 2,
+            dma((2,)),
             *[dma((2, 4))] * 4,
-            *[dma((32,))] * 4,
+            *[dma((16,))] * 2,
+            *[dma((32,))] * 2,
             *[dma((1,))] * 2,
             *[dma((16,))] * 2,
             *[dma((8,))] * 2,
         ],
         compiler_params=pltpu.CompilerParams(collective_id=0, has_side_effects=True, vmem_limit_bytes=67_000_000),
     )(pre, delta, head_weight, client_ids)
+    head, bias, embed, span = pl.pallas_call(
+        scale,
+        name="scale",
+        out_shape=(
+            jax.ShapeDtypeStruct((LANES, here), f32),
+            jax.ShapeDtypeStruct((1, here), f32),
+            jax.ShapeDtypeStruct((clients, here), f32),
+            jax.ShapeDtypeStruct((spans, here), f32),
+        ),
+        in_specs=[in_vmem] * 4,
+        out_specs=[in_vmem] * 4,
+    )(head, rest, embed, total)
     return head, bias[0], embed, span
 
 

time: 80.4 us -> 72.8 us (0.905)
  local copies, waits for them, and re-layouts: 6.35 us -> 0 us
  Pallas kernels: 73.1 us -> 72 us
    unnamed x4 -> x0, local copies, waits for them, and re-layouts: 6.35 us -> none
    pallas_call x1, Pallas kernels: 73.1 us -> 69.8 us  [per_device(): pl.pallas_call(kernel, name='products', out_shape=(jax.ShapeDtypeStruct((...]
    pallas_call x0 -> x1, Pallas kernels: none -> 2.21 us  [per_device(): pl.pallas_call(scale, name='scale', out_shape=(jax.ShapeDtypeStruct((LANE...]
where the time goes in v3:
time: 72.8 us; the launch traced here: 72.7 us
  Pallas kernels  72 us (99%)
    pallas_call x1, Pallas kernels, per_device(): pl.pallas_call(kernel, name='products', out_shape=(jax.ShapeDtypeStruct((...  69.8 us
    pallas_call x1, Pallas kernels, per_device(): pl.pallas_call(scale, name='scale', out_shape=(jax.ShapeDtypeStruct((LANE...  2.21 us

profile of v3, /device:TPU:1, one launch (start us, length us, event | category | flops | bytes accessed | tf_op | source)
XLA Modules:
  0.0 72.7 jit_solution(8680165888544411965)
XLA Ops:
  0.6 69.8 %products.1 = (f32[128,1024]{1,0:T(8,128)}, bf16[96,1024]{1,0:T(8,128)(2,1)}, f32[16,1024]{1,0:T(8,128)}, f32[8,128]{1,0:T(8,128)}) custom-call(bf16[1280,4096]{1,0:T(8,128)(2,1)} %pre_hbm.1, f32[1280,1024]{1,0:T(8,128)} %delta_hbm.1, bf16[4096,1024]{1,0:T(8,128)(2,1)} %weight_hbm.1, s32[16]{0:T(128)} %ids_ref.1), custom_call_target="tpu_custom_call" | custom-call | tf_op jit(solution)/shard_map/products/pallas_call | solution.py:517
  70.5 2.2 %scale.1 = (f32[128,1024]{1,0:T(8,128)}, f32[1,1024]{1,0:T(1,128)}, f32[16,1024]{1,0:T(8,128)}, f32[80,1024]{1,0:T(8,128)}) custom-call(f32[128,1024]{1,0:T(8,128)} %get-tuple-element.12.head, bf16[96,1024]{1,0:T(8,128)(2,1)} %get-tuple-element.13.rest, f32[16,1024]{1,0:T(8,128)} %get-tuple-element.14.embed, f32[8,128]{1,0:T(8,128)} %get-tuple-element.15.total), custom_call_target="tpu_custom_call" | custom-call | tf_op jit(solution)/shard_map/scale/pallas_call | solution.py:583

commit v4 on v3

--- a/solution.py
+++ b/solution.py
@@ -23,7 +23,7 @@
 
 def kernel(
     pre_hbm, delta_hbm, weight_hbm, ids_ref, head_out, rest_out, embed_out, total_out,
-    stage, low, low_t, weight, pre_b, hid_a, hid_b, slope, prod, crecv, acc_a, acc_b, sums, span_low, rows_low, span_in, rows_in, own_send, own_in, bias_rows, r_a, r_b, r_a2, r_b2,
+    stage, low, low_t, weight, pre_b, hid_a, hid_b, slope_a, slope_b, prod, crecv, acc_a, acc_b, sums, span_low, rows_low, span_in, rows_in, own_send, own_in, bias_rows, r_a, r_b, r_a2, r_b2,
     ids, emb, rest_own, rest_in, rest_all, picked, picked_in, squares, squares_zx, squares_y,
     delta_sem, weight_sem, pre_sem, c_send, c_recv, a_send, a_recv, b_send, b_recv, a2_send, a2_recv, b2_send, b2_recv, y_send, y_recv, ys_send, ys_recv, own_sems,
     i_send, i_recv, e_send, e_recv, rs_send, rs_recv, ag_send, ag_recv, p_send, p_recv, zx_send, zx_recv, sy_send, sy_recv,
@@ -95,8 +95,8 @@
             value = v * gate
             hid[lines, :] = value.astype(jnp.bfloat16)
             slant = (gate + value * (1.0 - gate)).astype(jnp.bfloat16)
-            for h in range(2):
-                slope[at[h], lines, pl.ds(h * LANES, LANES)] = slant[:, h * LANES : (h + 1) * LANES]
+            slope_a[at[0], lines, :] = slant[:, :LANES]
+            slope_b[at[1], lines, :] = slant[:, LANES:]
 
     def remote(src, dst, send, recv, to):
         return pltpu.make_async_remote_copy(src_ref=src, dst_ref=dst, send_sem=send, recv_sem=recv, device_id=to, device_id_type=MESH)
@@ -359,13 +359,15 @@
     lax.fori_loop(0, STEPS // 2, first_product, tuple(jnp.int32(t) for t in (next_p, next_q, load_p, load_q)))
 
     def reduce_rows(acc, chunk, u):
-        span = jnp.zeros((spans, BLOCK), jnp.float32)
-        for client in range(clients):
-            lines = pl.ds(client * spans, spans)
-            grad = acc[lines, :] * slope[chunk, lines, :].astype(jnp.float32)
-            span = span + grad
-            sums[u, pl.ds(spans + client, 1), :] = jnp.sum(grad, axis=0, keepdims=True)
-        sums[u, pl.ds(0, spans), :] = span
+        for h, slope in enumerate((slope_a, slope_b)):
+            lanes = pl.ds(h * LANES, LANES)
+            span = jnp.zeros((spans, LANES), jnp.float32)
+            for client in range(clients):
+                lines = pl.ds(client * spans, spans)
+                grad = acc[lines, lanes] * slope[chunk, lines, :].astype(jnp.float32)
+                span = span + grad
+                sums[u, pl.ds(spans + client, 1), lanes] = jnp.sum(grad, axis=0, keepdims=True)
+            sums[u, pl.ds(0, spans), lanes] = span
 
     for part in range(4):
         weight_copy(part).wait()
@@ -533,7 +535,8 @@
             pltpu.VMEM((4, rows, BLOCK), bf16),
             pltpu.VMEM((rows, BLOCK), bf16),
             pltpu.VMEM((rows, BLOCK), bf16),
-            pltpu.VMEM((STEPS + 1, rows, BLOCK), bf16),
+            pltpu.VMEM((STEPS + 1, rows, LANES), bf16),
+            pltpu.VMEM((STEPS + 1, rows, LANES), bf16),
             pltpu.VMEM((STEPS, 2, here, LANES), bf16),
             pltpu.VMEM((STEPS, here, LANES), bf16),
             pltpu.VMEM((rows, BLOCK), f32),

time: 72.8 us -> 71 us (0.975)
  Pallas kernels: 72 us -> 70.2 us
    pallas_call x1, Pallas kernels: 69.8 us -> 68 us  [per_device(): pl.pallas_call(kernel, name='products', out_shape=(jax.ShapeDtypeStruct((...]
where the time goes in v4:
time: 71 us; the launch traced here: 70.8 us
  Pallas kernels  70.2 us (99%)
    pallas_call x1, Pallas kernels, per_device(): pl.pallas_call(kernel, name='products', out_shape=(jax.ShapeDtypeStruct((...  68 us
    pallas_call x1, Pallas kernels, per_device(): pl.pallas_call(scale, name='scale', out_shape=(jax.ShapeDtypeStruct((LANE...  2.21 us

profile of v4, /device:TPU:1, one launch (start us, length us, event | category | flops | bytes accessed | tf_op | source)
XLA Modules:
  0.0 70.8 jit_solution(11975541516260474378)
XLA Ops:
  0.6 68.0 %products.1 = (f32[128,1024]{1,0:T(8,128)}, bf16[96,1024]{1,0:T(8,128)(2,1)}, f32[16,1024]{1,0:T(8,128)}, f32[8,128]{1,0:T(8,128)}) custom-call(bf16[1280,4096]{1,0:T(8,128)(2,1)} %pre_hbm.1, f32[1280,1024]{1,0:T(8,128)} %delta_hbm.1, bf16[4096,1024]{1,0:T(8,128)(2,1)} %weight_hbm.1, s32[16]{0:T(128)} %ids_ref.1), custom_call_target="tpu_custom_call" | custom-call | tf_op jit(solution)/shard_map/products/pallas_call | solution.py:519
  68.6 2.2 %scale.1 = (f32[128,1024]{1,0:T(8,128)}, f32[1,1024]{1,0:T(1,128)}, f32[16,1024]{1,0:T(8,128)}, f32[80,1024]{1,0:T(8,128)}) custom-call(f32[128,1024]{1,0:T(8,128)} %get-tuple-element.12.head, bf16[96,1024]{1,0:T(8,128)(2,1)} %get-tuple-element.13.rest, f32[16,1024]{1,0:T(8,128)} %get-tuple-element.14.embed, f32[8,128]{1,0:T(8,128)} %get-tuple-element.15.total), custom_call_target="tpu_custom_call" | custom-call | tf_op jit(solution)/shard_map/scale/pallas_call | solution.py:586
